TPU v7x, 512 devices: a whole 4x8x8 slice. The times are simulated.
512 devices in a mesh: band: 16 (over y, z_lo), ga: 32 (over x, z_hi, core).
Axes of the slice: x: 4, y: 8, z: 8 (z_hi: 4, z_lo: 2; z = z_hi * 2 + z_lo), core: 2. Of those that a mesh axis runs over, the one named last changes fastest.
Arguments:
- orbitals: bfloat16 [32768, 4096], P('ga', 'band'), may hold values from -6 to 6
Outputs:
- margin: float32 [4096, 4096], P('band', 'ga')
- corrected: bfloat16 [32768, 4096], P('ga', 'band')
All inputs are finite; a program needn't handle non-finite values.
Results may differ from a plain program's by a relative error of at most 0.0056.
Values may be sent and summed in bfloat16 or wider, within the bound.
A program may use at most 64 MiB of HBM per device.

v0:
```python
import jax
import jax.numpy as jnp
from jax import lax
from jax.sharding import Mesh
from jax.sharding import PartitionSpec as P

BAND = ("band_0", "band_1")


def whole_of(value, axes, dim):
    if not axes:
        return value
    nearer = lax.all_gather(value, axes[-1], axis=dim, tiled=True)
    return whole_of(nearer, axes[:-1], dim)


def split_up(value, dim, count):
    before, after = (value.shape[:dim], value.shape[dim + 1 :])
    return jnp.moveaxis(value.reshape(*before, count, -1, *after), dim, 0)


def sum_at_owner(value, axis, dim):
    blocks = split_up(value, dim, lax.axis_size(axis))
    arrived = lax.all_to_all(blocks, axis, split_axis=0, concat_axis=0, tiled=True)
    return arrived.astype(jnp.float32).sum(axis=0)


def in_order(blocks, dim):
    dims = list(blocks.shape[1:])
    dims[dim] *= blocks.shape[0]
    return jnp.moveaxis(blocks, 0, dim).reshape(dims)


def sent_to_all(value, axis):
    count = lax.axis_size(axis)
    return lax.all_to_all(
        jnp.broadcast_to(value[None], (count, *value.shape)), axis, 0, 0, tiled=True
    )


def gathered_copies(value, axis, dim):
    return in_order(sent_to_all(value, axis), dim)


def identity_block(rows, cols, row_start, col_start):
    row_index = row_start + lax.iota(jnp.int32, rows)
    col_index = col_start + lax.iota(jnp.int32, cols)
    return (row_index[:, None] == col_index[None, :]).astype(jnp.float32)


def shards(orbitals):
    own_coeffs = orbitals.shape[0]
    own_bands = orbitals.shape[1]
    all_bands = own_bands * lax.axis_size(BAND)
    all_coeffs = own_coeffs * lax.axis_size("ga")
    col_width = all_bands // lax.axis_size("ga")
    row_start = lax.axis_index(BAND) * own_bands
    col_start = lax.axis_index("ga") * col_width
    everyone = whole_of(orbitals, BAND, 1)
    partial_value = lax.dot_general(
        orbitals, everyone, (((0,), (0,)), ((), ())), preferred_element_type=jnp.float32
    )
    unit_block = identity_block(own_bands, col_width, row_start, col_start)
    margin_block = sum_at_owner(partial_value.astype(jnp.bfloat16), "ga", 1) / all_coeffs
    deviation_block = margin_block - unit_block
    deviation_rows = lax.all_gather(
        deviation_block.astype(jnp.bfloat16), "ga", axis=1, tiled=True
    ).astype(deviation_block.dtype)
    deviation_cols = gathered_copies(deviation_block.astype(jnp.bfloat16), BAND, 0).astype(
        deviation_block.dtype
    )
    square = jnp.dot(
        deviation_rows,
        deviation_cols,
        precision=lax.Precision.HIGHEST,
        preferred_element_type=jnp.float32,
    )
    fix_block = (unit_block - 0.5 * deviation_block + 0.375 * square).astype(jnp.bfloat16)
    fix_rows = gathered_copies(fix_block, "ga", 1)
    corrected = lax.dot_general(
        everyone, fix_rows, (((1,), (1,)), ((), ())), preferred_element_type=jnp.float32
    )
    return (margin_block, corrected.astype(jnp.bfloat16))


def solution(mesh):
    finer = Mesh(mesh.devices.reshape(8, 2, mesh.shape["ga"]), ("band_0", "band_1", "ga"))
    placed = (P("ga", BAND),)
    return jax.shard_map(
        shards,
        mesh=finer,
        in_specs=placed,
        out_specs=(P(BAND, "ga"), P("ga", BAND)),
        check_vma=False,
    )
```

profile of v0, /device:TPU:1, one launch (start us, length us, event | category | flops | bytes accessed | tf_op | source)
XLA Modules:
  0.0 347.4 jit_solution(5040010379792881687)
XLA Ops:
  7.2 0.0 all-gather.4.cloned.1.call-start
  7.2 0.7 all-gather.4.cloned.1.call-update
  7.9 0.0 all-gather.6.cloned.1.call-start
  7.9 36.7 %all-gather.4.cloned.1.call-done = bf16[1024,512]{1,0:T(8,128)(2,1)} async-done(((bf16[1024,256]{1,0:T(8,128)(2,1)}), bf16[1024,512]{1,0:T(8,128)(2,1)}) %all-gather.4.cloned.1.call-update) | async-done | bytes 1048592 | tf_op jit(solution)/shard_map/all_gather | solution.py:13
  44.7 0.0 all-gather.6.cloned.1.call-update
  44.7 98.9 %all-gather.6.cloned.1.call-done = bf16[1024,4096]{1,0:T(8,128)(2,1)} async-done(((bf16[1024,512]{1,0:T(8,128)(2,1)}), bf16[1024,4096]{1,0:T(8,128)(2,1)}) %all-gather.6.cloned.1.call-update) | async-done | bytes 8388624 | tf_op jit(solution)/shard_map/all_gather | solution.py:13
  143.6 6.0 %fusion = bf16[32,32,8,128]{3,2,1,0:T(8,128)(2,1)S(1)} fusion(bf16[1024,256]{1,0:T(8,128)(2,1)} %param.1, bf16[1024,4096]{1,0:T(8,128)(2,1)} %all-gather.6.cloned.1.call-done), kind=kOutput, calls=%fused_computation.3 | convolution fusion | flops 2148532224 | bytes 11010048 | tf_op jit(solution)/shard_map/dot_general | solution.py:60
  149.6 1.9 copy.11
  151.5 10.8 %all-to-all-start = ((bf16[32,256,128]{2,1,0:T(8,128)(2,1)}), bf16[32,256,128]{2,1,0:T(8,128)(2,1)S(1)}, u32[]{:S(2)}, u32[]{:S(2)}) async-start(bf16[32,256,128]{2,1,0:T(8,128)(2,1)} %bitcast.20), calls=%async_computation | async-start | bytes 4194304 | tf_op jit(solution)/shard_map/all_to_all | solution.py:24
  162.3 0.0 all-gather.8.cloned.1.call-start
  162.4 51.7 %all-to-all-done = bf16[32,256,128]{2,1,0:T(8,128)(2,1)S(1)} async-done(((bf16[32,256,128]{2,1,0:T(8,128)(2,1)}), bf16[32,256,128]{2,1,0:T(8,128)(2,1)S(1)}, u32[]{:S(2)}, u32[]{:S(2)}) %all-to-all-start) | async-done | bytes 2097184 | tf_op jit(solution)/shard_map/all_to_all | solution.py:24
  214.0 0.3 convert_reduce_fusion
  214.3 0.7 fusion.4
  215.1 0.0 copy-start
  215.1 0.0 all-gather.8.cloned.1.call-update
  215.1 1.1 broadcast_in_dim.4
  216.2 30.9 %all_to_all.15 = bf16[16,256,128]{2,1,0:T(8,128)(2,1)S(1)} all-to-all(bf16[16,256,128]{2,1,0:T(8,128)(2,1)S(1)} %broadcast_in_dim.4), channel_id=1, replica_groups=mesh['band_0'=8,'band_1'=2,'ga'=32] {'band_0','band_1'}, dimensions={0} | all-to-all | bytes 2097152 | tf_op jit(solution)/shard_map/all_to_all | solution.py:36
  247.1 27.0 %all-gather.8.cloned.1.call-done = bf16[256,4096]{1,0:T(8,128)(2,1)} async-done(((bf16[256,128]{1,0:T(8,128)(2,1)}), bf16[256,4096]{1,0:T(8,128)(2,1)}) %all-gather.8.cloned.1.call-update) | async-done | bytes 2097168 | tf_op jit(solution)/shard_map/all_gather | solution.py:66
  274.1 2.3 fusion.3
  276.4 0.0 copy-done
  276.4 0.1 copy.7
  276.5 0.2 broadcast_in_dim.5
  276.8 57.4 %all_to_all.16 = bf16[32,256,128]{1,2,0:T(8,128)(2,1)S(1)} all-to-all(bf16[32,256,128]{1,2,0:T(8,128)(2,1)S(1)} %broadcast_in_dim.5), channel_id=1, replica_groups=mesh['band_0'=8,'band_1'=2,'ga'=32] {'ga'}, dimensions={0} | all-to-all | bytes 4194304 | tf_op jit(solution)/shard_map/all_to_all | solution.py:36
  334.1 5.8 %fusion.1 = bf16[1024,256]{0,1:T(8,128)(2,1)S(1)} fusion(bf16[256,4096]{0,1:T(8,128)(2,1)S(1)} %bitcast.22, bf16[1024,4096]{1,0:T(8,128)(2,1)} %all-gather.6.cloned.1.call-done), kind=kOutput, calls=%fused_computation.5 | convolution fusion | flops 2147745792 | bytes 11010048 | tf_op jit(solution)/shard_map/dot_general | solution.py:80
  339.9 1.0 copy.8
  (2 shorter events, 0.0 us)
Async XLA Ops:
  7.2 37.5 %all-gather.4.cloned.1.call-start = ((), (), s32[]{:S(2)}) async-start(), calls=%async_computation.3 | async-start | bytes 1572864 | tf_op jit(solution)/shard_map/all_gather | solution.py:13
  7.9 135.7 %all-gather.6.cloned.1.call-start = ((), (), s32[]{:S(2)}) async-start(), calls=%async_computation.4 | async-start | bytes 9437184 | tf_op jit(solution)/shard_map/all_gather | solution.py:13
  151.5 62.5 %all-to-all-start = ((bf16[32,256,128]{2,1,0:T(8,128)(2,1)}), bf16[32,256,128]{2,1,0:T(8,128)(2,1)S(1)}, u32[]{:S(2)}, u32[]{:S(2)}) async-start(bf16[32,256,128]{2,1,0:T(8,128)(2,1)} %bitcast.20), calls=%async_computation | async-start | bytes 4194304 | tf_op jit(solution)/shard_map/all_to_all | solution.py:24
  162.3 111.8 %all-gather.8.cloned.1.call-start = ((), (), s32[]{:S(2)}) async-start(), calls=%async_computation.5 | async-start | bytes 2162688 | tf_op jit(solution)/shard_map/all_gather | solution.py:66
  215.1 61.4 %copy-start = (f32[256,128]{1,0:T(8,128)}, f32[256,128]{1,0:T(8,128)S(1)}, u32[]{:S(2)}) copy-start(f32[256,128]{1,0:T(8,128)S(1)} %get-tuple-element.9) | copy-start | bytes 393220
Sparse Core Ops, SparseCore 0:
  10.0 34.5 all-gather.3
  46.8 96.7 all-gather.5
  215.2 58.8 all-gather.7
where the time goes:
time: 348 us; the launch traced here: 347 us
  waiting for transfers between devices  215 us (62%)
  blocking collectives  88.3 us (25%)
  matrix products  14 us (4%)
  between operations  13.8 us (4%)
  starting transfers between devices  10.9 us (3%)
  local copies, waits for them, and re-layouts  4.35 us (1%)
    all_gather x2, waiting for transfers between devices, whole_of(): nearer = lax.all_gather(value, axes[-1], axis=dim, tiled=True)  136 us
    all_to_all x2, blocking collectives, sent_to_all(): lax.all_to_all(jnp.broadcast_to(value[None], (count, *value.shape)), axis...  88.3 us
    all_to_all x1, waiting for transfers between devices, sum_at_owner(): lax.all_to_all(blocks, axis, split_axis=0, concat_axis=0, tiled=True)  51.7 us
    all_gather x1, waiting for transfers between devices, shards(): lax.all_gather(deviation_block.astype(jnp.bfloat16), 'ga', axis=1, tiled=...  27 us
    all_to_all x1, starting transfers between devices, sum_at_owner(): lax.all_to_all(blocks, axis, split_axis=0, concat_axis=0, tiled=True)  10.8 us
  transfers between devices with their start and end apart: 4, of which 4 were waited for; matrix products, arithmetic and copies ran while one was open for 0% of the time, Pallas kernels for 0%

commit v1 on v0

v1 whole, which is shorter than its diff:
```python
import jax
import jax.numpy as jnp
from jax import lax
from jax.experimental import pallas as pl
from jax.experimental.pallas import tpu as pltpu
from jax.sharding import Mesh
from jax.sharding import PartitionSpec as P

AXES = ("y", "zl", "x", "zh", "c")
NY, NX, NZ = 8, 4, 8
SLOT = (0, 1, 7, 2, 6, 3, 5, 4)
POS = tuple(SLOT.index(k) for k in range(NY))
GROUPS = ((0, 3), (3, 2), (5, 2), (7, 1))
MESH_ID = pl.DeviceIdType.MESH
F32 = jnp.float32
BF16 = jnp.bfloat16


def dot(a, b, dims=(((1,), (0,)), ((), ()))):
    return lax.dot_general(a, b, dims, preferred_element_type=F32)


def kernel(
    total_rows, x_hbm, m_out, o_out, xa, ph, xs, xr, zs, zr, db, d32, dj, da, dbb, cb, ca, cbb,
    ms, mr, acc, osb, in_sem, sw_s, sw_r, ring_s, ring_r, sib_s, sib_r, x_s, x_r, z_s, z_r,
    y_s, y_r, yf_s, yf_r, ax_s, ax_r, az_s, az_r, bz_s, bz_r, bx_s, bx_r, m_s, m_r, out_s, out_r,
):
    y = lax.axis_index("y")
    zl = lax.axis_index("zl")
    x = lax.axis_index("x")
    zh = lax.axis_index("zh")
    c = lax.axis_index("c")
    z = zh * 2 + zl
    half = ph.shape[0]
    band = ph.shape[1]
    xrows = xs.shape[2]
    zrows = zs.shape[2]
    sends = []

    def zdev(d):
        t = lax.rem(z + d + NZ, NZ)
        return {"zh": t // 2, "zl": lax.rem(t, 2)}

    def ydev(d):
        return {"y": lax.rem(y + d + NY, NY)}

    def xdev(d):
        return {"x": lax.rem(x + d + NX, NX)}

    sibling = {"c": 1 - c}

    def copy(src, dst, ssem, rsem, dev):
        return pltpu.make_async_remote_copy(
            src_ref=src, dst_ref=dst, send_sem=ssem, recv_sem=rsem, device_id=dev, device_id_type=MESH_ID
        )

    def send(src, dst, ssem, rsem, dev):
        h = copy(src, dst, ssem, rsem, dev)
        h.start()
        sends.append(h)

    def arrived(dst, ssem, rsem):
        copy(dst, dst, ssem, rsem, sibling).wait_recv()

    own_in = pltpu.make_async_copy(x_hbm.at[pl.ds(zl * half, half), :], xa.at[0, c, zl], in_sem.at[0])
    oth_in = pltpu.make_async_copy(x_hbm.at[pl.ds((1 - zl) * half, half), :], ph, in_sem.at[1])
    own_in.start()
    oth_in.start()

    barrier = pltpu.get_barrier_semaphore()
    peers = [sibling, {"zl": 1 - zl, "c": 1 - c}]
    peers += [ydev(d) for d in range(1, NY)]
    peers += [xdev(d) for d in range(1, NX)]
    peers += [zdev(d) for d in range(1, NZ)]
    for dev in peers:
        pl.semaphore_signal(barrier, inc=1, device_id=dev, device_id_type=MESH_ID)
    pl.semaphore_wait(barrier, len(peers))

    oth_in.wait()
    own_in.wait()
    send(ph, xa.at[0, c, zl], sw_s, sw_r, {"zl": 1 - zl})

    subs = (zl, 1 - zl)

    def to_minus(k, j):
        t = xa.at[k, c, subs[j]]
        u = xa.at[k + 1, c, subs[j]]
        send(t, u, ring_s.at[0, k, j], ring_r.at[0, k, j], ydev(-1))

    def to_plus(k, j):
        t = xa.at[(NY - k) % NY, c, subs[j]]
        u = xa.at[NY - k - 1, c, subs[j]]
        send(t, u, ring_s.at[1, k, j], ring_r.at[1, k, j], ydev(1))

    def to_sibling(k, j):
        t = xa.at[k, c, subs[j]]
        send(t, t, sib_s.at[k, j], sib_r.at[k, j], sibling)

    def from_sibling(k):
        for j in range(2):
            arrived(xa.at[k, 1 - c, subs[j]], sib_s.at[k, j], sib_r.at[k, j])

    def partial_margin(g):
        off, n = GROUPS[g]
        for p in range(off, off + n):
            k = SLOT[p]
            for s in range(2):
                v = dot(xa[k, 0, s], xa[0, 0, c], (((0,), (0,)), ((), ())))
                v = v + dot(xa[k, 1, s], xa[0, 1, c], (((0,), (0,)), ((), ())))
                v = v.astype(BF16)
                xs[2 * s, p] = v[:xrows]
                xs[2 * s + 1, p] = v[xrows:]
        for d in range(1, NX):
            dev = xdev(d)
            send(
                xs.at[dev["x"], pl.ds(off, n)], xr.at[d - 1, pl.ds(off, n)],
                x_s.at[g, d - 1], x_r.at[g, d - 1], dev,
            )

    def sum_over_x(g):
        off, n = GROUPS[g]
        for d in range(1, NX):
            arrived(xr.at[d - 1, pl.ds(off, n)], x_s.at[g, d - 1], x_r.at[g, d - 1])
        for p in range(off, off + n):
            v = xs[x, p].astype(F32)
            for d in range(1, NX):
                v = v + xr[d - 1, p].astype(F32)
            zs[:, p] = v.astype(BF16).reshape(NZ, zrows, band)
        for d in range(1, NZ):
            t = lax.rem(z + d, NZ)
            send(
                zs.at[t, pl.ds(off, n)], zr.at[d - 1, pl.ds(off, n)],
                z_s.at[g, d - 1], z_r.at[g, d - 1], zdev(d),
            )

    def sum_over_z(g):
        off, n = GROUPS[g]
        for d in range(1, NZ):
            arrived(zr.at[d - 1, pl.ds(off, n)], z_s.at[g, d - 1], z_r.at[g, d - 1])
        for p in range(off, off + n):
            v = zs[z, p].astype(F32)
            for d in range(1, NZ):
                v = v + zr[d - 1, p].astype(F32)
            v = v * (1.0 / total_rows)
            if p == 0:
                v = v - unit(zrows, band, x * xrows + z * zrows, c * band)
            d32[p] = v
            w = v.astype(BF16)
            db[p] = w
            put_own(da, dbb, p, w)

    def unit(rows, cols, row0, col0):
        i = lax.broadcasted_iota(jnp.int32, (rows, cols), 0) + row0
        j = lax.broadcasted_iota(jnp.int32, (rows, cols), 1) + col0
        return (i == j).astype(F32)

    def put_own(a, b, p, w):
        if p < 4:
            a[z, x, p] = w
        else:
            b[x, z, p - 4] = w

    for j in range(2):
        if j == 1:
            arrived(xa.at[0, c, 1 - zl], sw_s, sw_r)
        to_minus(0, j)
        to_plus(0, j)
        to_sibling(0, j)
    for h in range(1, 5):
        for j in range(2):
            if h < 4 or j == 0:
                arrived(xa.at[h, c, subs[j]], ring_s.at[0, h - 1, j], ring_r.at[0, h - 1, j])
                if h < 3 or (h == 3 and j == 0):
                    to_minus(h, j)
                to_sibling(h, j)
            if h < 4 or j == 1:
                arrived(xa.at[NY - h, c, subs[j]], ring_s.at[1, h - 1, j], ring_r.at[1, h - 1, j])
                if h < 3 or (h == 3 and j == 1):
                    to_plus(h, j)
                to_sibling(NY - h, j)
        if h == 1:
            from_sibling(0)
        from_sibling(h)
        if h < 4:
            from_sibling(NY - h)
        partial_margin(h - 1)
        if h > 1:
            sum_over_x(h - 2)
        if h > 2:
            sum_over_z(h - 3)
    sum_over_x(3)
    sum_over_z(2)
    sum_over_z(3)

    def plane_gather(q, a, b, between, a_done):
        def az(i, h):
            t = lax.rem(z + (h if i == 0 else NZ - h), NZ)
            if h < 4:
                return a.at[t]
            return a.at[t, pl.ds(2 * i, 2)]

        def bz(i, h):
            t = lax.rem(z + (h if i == 0 else NZ - h), NZ)
            if h < 4:
                return b.at[x, t]
            return b.at[x, t, pl.ds(2 * i, 2)]

        def ring(blk, i, h, ss, rs):
            t = lax.rem(z + (h - 1 if i == 0 else NZ - h + 1), NZ)
            if blk == 0:
                v = a.at[t] if h < 4 else a.at[t, pl.ds(2 * i, 2)]
            else:
                v = b.at[x, t] if h < 4 else b.at[x, t, pl.ds(2 * i, 2)]
            send(v, v, ss.at[q, i, h - 1], rs.at[q, i, h - 1], zdev(-1 if i == 0 else 1))

        for d in range(1, NX):
            send(a.at[z, x], a.at[z, x], ax_s.at[q, d - 1], ax_r.at[q, d - 1], xdev(d))
        for i in range(2):
            ring(1, i, 1, bz_s, bz_r)

        def b_hop(h):
            for i in range(2):
                arrived(bz(i, h), bz_s.at[q, i, h - 1], bz_r.at[q, i, h - 1])
                if h < 4:
                    ring(1, i, h + 1, bz_s, bz_r)

        def a_hop(h):
            for i in range(2):
                arrived(az(i, h), az_s.at[q, i, h - 1], az_r.at[q, i, h - 1])
                if h < 4:
                    ring(0, i, h + 1, az_s, az_r)

        b_hop(1)
        for d in range(1, NX):
            t = lax.rem(x + NX - d, NX)
            arrived(a.at[z, t], ax_s.at[q, d - 1], ax_r.at[q, d - 1])
        for i in range(2):
            ring(0, i, 1, az_s, az_r)
        b_hop(2)
        b_hop(3)
        a_hop(1)
        b_hop(4)
        for i in range(2):
            send(b.at[x], b.at[x], bx_s.at[q, i, 0], bx_r.at[q, i, 0], xdev(-1 if i == 0 else 1))
        between()
        a_hop(2)
        a_hop(3)
        for i in range(2):
            t = lax.rem(x + (1 if i == 0 else NX - 1), NX)
            arrived(b.at[t], bx_s.at[q, i, 0], bx_r.at[q, i, 0])
            v = b.at[t, pl.ds(4 * i, 4)]
            send(v, v, bx_s.at[q, i, 1], bx_r.at[q, i, 1], xdev(-1 if i == 0 else 1))
        a_hop(4)
        a_done()
        for i in range(2):
            t = lax.rem(x + 2, NX)
            arrived(b.at[t, pl.ds(4 * i, 4)], bx_s.at[q, i, 1], bx_r.at[q, i, 1])

    dj[0, c] = db[...].reshape(NY * zrows, band)
    send(dj.at[0, c], dj.at[0, c], yf_s.at[0], yf_r.at[0], sibling)
    for k in range(1, NY):
        send(dj.at[0, c], dj.at[k, c], y_s.at[k - 1], y_r.at[k - 1], ydev(-k))

    def pass_on():
        for k in range(1, NY):
            arrived(dj.at[k, c], y_s.at[k - 1], y_r.at[k - 1])
            send(dj.at[k, c], dj.at[k, c], yf_s.at[k], yf_r.at[k], sibling)

    plane_gather(0, da, dbb, pass_on, lambda: None)
    for k in range(NY):
        arrived(dj.at[k, 1 - c], yf_s.at[k], yf_r.at[k])

    def quarter(a, b, p, q):
        v = a[:, q, p] if p < 4 else b[q, :, p - 4]
        return v.reshape(xrows, band)

    def rows_of(a, b, p, s):
        return jnp.concatenate([quarter(a, b, p, 2 * s), quarter(a, b, p, 2 * s + 1)], axis=0)

    acc_sq = [None] * NY
    for k in range(NY):
        part = dot(dj[k, 0], rows_of(da, dbb, POS[k], 0)) + dot(dj[k, 1], rows_of(da, dbb, POS[k], 1))
        for p in range(NY):
            m = POS[(k + SLOT[p]) % NY]
            piece = part[p * zrows : (p + 1) * zrows]
            acc_sq[m] = piece if acc_sq[m] is None else acc_sq[m] + piece
    for p in range(NY):
        v = 0.375 * acc_sq[p] - 0.5 * d32[p]
        if p == 0:
            v = v + unit(zrows, band, x * xrows + z * zrows, c * band)
        put_own(ca, cbb, p, v.astype(BF16))

    kg = lax.rem(x * 2 + zh // 2 - y + NY, NY)
    pg = jnp.where(kg == 0, 0, jnp.where(kg <= 4, 2 * kg - 1, 2 * (NY - kg)))
    pa = jnp.minimum(pg, 3)
    pb = jnp.maximum(pg - 4, 0)

    def mirror(core):
        q = lax.rem(zh, 2) * 2 + core
        va = da[:, q, pa].reshape(xrows, band)
        vb = dbb[q, :, pb].reshape(xrows, band)
        return jnp.where(pg < 4, va.astype(F32), vb.astype(F32))

    def margin_work():
        ms[...] = mirror(1 - c).astype(BF16)
        send(ms, mr, m_s, m_r, sibling)

    def product(part):
        for cc in range(2):
            for p in range(4 * part, 4 * part + 4):
                k = SLOT[p]
                for s in range(2):
                    v = dot(xa[k, cc, s], rows_of(ca, cbb, p, s))
                    if part == 0 and p == 0 and s == 0:
                        acc[cc] = v
                    else:
                        acc[cc] += v
            if part == 1:
                osb[cc] = acc[cc].astype(BF16)
                mine = (zl == c) & (c == cc)
                to = copy(
                    osb.at[cc], o_out.at[pl.ds(zl * half, half), :], out_s.at[cc], out_r.at[zl], {"zl": c, "c": cc}
                )

                @pl.when(jnp.logical_not(mine))
                def _():
                    to.start()

                @pl.when(mine)
                def _():
                    o_out[pl.ds(pl.multiple_of(zl * half, half), half), :] = osb[cc]

    def first_half():
        arrived(mr, m_s, m_r)
        v = jnp.where(zl == c, mirror(c), mr[...].astype(F32))
        rows0 = (y * 2 + zl) * band
        cols0 = (x * 8 + zh * 2 + c) * xrows
        m_out[...] = v.T + unit(band, xrows, rows0, cols0)
        product(0)

    plane_gather(1, ca, cbb, margin_work, first_half)
    product(1)

    other = o_out.at[pl.ds((1 - zl) * half, half), :]
    arrived(other, out_s.at[0], out_r.at[1 - zl])

    @pl.when(zl != c)
    def _():
        arrived(o_out.at[pl.ds(zl * half, half), :], out_s.at[0], out_r.at[zl])

    for cc in range(2):

        @pl.when(jnp.logical_not((zl == c) & (c == cc)))
        def _():
            copy(
                osb.at[cc], o_out.at[pl.ds(zl * half, half), :], out_s.at[cc], out_r.at[zl], {"zl": c, "c": cc}
            ).wait_send()

    for h in sends:
        h.wait_send()


def shards(total_rows, orbitals):
    rows, band = orbitals.shape
    half = rows // 2
    xrows = 2 * band // NX
    zrows = xrows // NZ
    dma = pltpu.SemaphoreType.DMA
    v = pltpu.VMEM
    scratch = [
        v((NY, 2, 2, half, band), BF16),
        v((half, band), BF16),
        v((NX, NY, xrows, band), BF16),
        v((NX - 1, NY, xrows, band), BF16),
        v((NZ, NY, zrows, band), BF16),
        v((NZ - 1, NY, zrows, band), BF16),
        v((NY, zrows, band), BF16),
        v((NY, zrows, band), F32),
        v((NY, 2, NY * zrows, band), BF16),
        v((NZ, NX, 4, zrows, band), BF16),
        v((NX, NZ, 4, zrows, band), BF16),
        v((NY, zrows, band), BF16),
        v((NZ, NX, 4, zrows, band), BF16),
        v((NX, NZ, 4, zrows, band), BF16),
        v((xrows, band), BF16),
        v((xrows, band), BF16),
        v((2, half, band), F32),
        v((2, half, band), BF16),
        dma((2,)),
        dma, dma,
        dma((2, 4, 2)), dma((2, 4, 2)),
        dma((NY, 2)), dma((NY, 2)),
        dma((4, NX - 1)), dma((4, NX - 1)),
        dma((4, NZ - 1)), dma((4, NZ - 1)),
        dma((NY - 1,)), dma((NY - 1,)),
        dma((NY,)), dma((NY,)),
        dma((2, NX - 1)), dma((2, NX - 1)),
        dma((2, 2, 4)), dma((2, 2, 4)),
        dma((2, 2, 4)), dma((2, 2, 4)),
        dma((2, 2, 2)), dma((2, 2, 2)),
        dma, dma,
        dma((2,)), dma((2,)),
    ]

    def body(*refs):
        kernel(total_rows, *refs)

    return pl.pallas_call(
        body,
        out_shape=(
            jax.ShapeDtypeStruct((band, xrows), F32),
            jax.ShapeDtypeStruct((rows, band), BF16),
        ),
        in_specs=[pl.BlockSpec(memory_space=pl.ANY)],
        out_specs=(pl.BlockSpec(memory_space=pltpu.VMEM), pl.BlockSpec(memory_space=pltpu.VMEM)),
        scratch_shapes=scratch,
        compiler_params=pltpu.CompilerParams(
            collective_id=0, has_side_effects=True, vmem_limit_bytes=56 * 1024 * 1024
        ),
    )(orbitals)


def solution(mesh):
    finer = Mesh(mesh.devices.reshape(NY, 2, NX, NZ // 2, 2), AXES)
    coeffs = ("x", "zh", "c")
    bands = ("y", "zl")

    def run(orbitals):
        total = orbitals.shape[0]
        return jax.shard_map(
            lambda o: shards(total, o),
            mesh=finer,
            in_specs=(P(coeffs, bands),),
            out_specs=(P(bands, coeffs), P(coeffs, bands)),
            check_vma=False,
        )(orbitals)

    return run
```

time: 348 us -> 139 us (0.40)
  waiting for transfers between devices: 215 us -> 0 us
  Pallas kernels: 0 us -> 135 us
  blocking collectives: 88.3 us -> 0 us
  matrix products: 14 us -> 0 us
  between operations: 13.8 us -> 0.64 us
  starting transfers between devices: 10.9 us -> 0 us
    all_gather x3 -> x0, waiting for transfers between devices: 163 us -> none  [the longest x2 136 us: whole_of(): nearer = lax.all_gather(value, axes[-1], axis=dim, tiled=True)]
    pallas_call x0 -> x1, Pallas kernels: none -> 135 us  [shards(): pl.pallas_call(body, out_shape=(jax.ShapeDtypeStruct((band, xrows), F32),...]
    all_to_all x2 -> x0, blocking collectives: 88.3 us -> none  [sent_to_all(): lax.all_to_all(jnp.broadcast_to(value[None], (count, *value.shape)), axis...]
    all_to_all x1 -> x0, waiting for transfers between devices: 51.7 us -> none  [sum_at_owner(): lax.all_to_all(blocks, axis, split_axis=0, concat_axis=0, tiled=True)]
    dot_general x3 -> x0, matrix products: 14 us -> none  [the longest x1 5.95 us: shards(): lax.dot_general(orbitals, everyone, (((0,), (0,)), ((), ())), preferred_e...]
    all_to_all x1 -> x0, starting transfers between devices: 10.8 us -> none  [sum_at_owner(): lax.all_to_all(blocks, axis, split_axis=0, concat_axis=0, tiled=True)]
  transfers between devices with their start and end apart: 4 -> 0, of which waited for: 4 -> 0; matrix products, arithmetic and copies ran while one was open for 0% -> 0% of each run, Pallas kernels for 0% -> 0%
where the time goes in v1:
time: 139 us
  Pallas kernels  135 us (97%)
  local copies, waits for them, and re-layouts  3.44 us (2%)
    pallas_call x1, Pallas kernels, shards(): pl.pallas_call(body, out_shape=(jax.ShapeDtypeStruct((band, xrows), F32),...  135 us
    unnamed x2, local copies, waits for them, and re-layouts  3.44 us

profile of v1, /device:TPU:1, one launch (start us, length us, event | category | flops | bytes accessed | tf_op | source)
XLA Modules:
  0.0 138.7 jit_solution(286574671078219282)
XLA Ops:
  0.6 134.6 %shard_map.30 = (f32[256,128]{1,0:T(8,128)}, bf16[1024,256]{1,0:T(8,128)(2,1)}) custom-call(bf16[1024,256]{1,0:T(8,128)(2,1)} %refs_0_.1), custom_call_target="tpu_custom_call" | custom-call | tf_op jit(solution)/shard_map/pallas_call | solution.py:408
  135.3 1.6 %copy.5 = f32[256,128]{1,0:T(8,128)} copy(f32[256,128]{1,0:T(8,128)} %get-tuple-element.4) | data formatting | bytes 262144
  136.8 1.9 %copy.6 = bf16[1024,256]{1,0:T(8,128)(2,1)} copy(bf16[1024,256]{1,0:T(8,128)(2,1)} %get-tuple-element.5) | data formatting | bytes 1048576

commit v2 on v1

--- a/solution.py
+++ b/solution.py
@@ -21,9 +21,10 @@
 
 
 def kernel(
-    total_rows, x_hbm, m_out, o_out, xa, ph, xs, xr, zs, zr, db, d32, dj, da, dbb, cb, ca, cbb,
+    total_rows, x_hbm, m_out, o_out, xa, ph, xs, xr, zs, zr, db, d32, dj, da, ca, cbb,
     ms, mr, acc, osb, in_sem, sw_s, sw_r, ring_s, ring_r, sib_s, sib_r, x_s, x_r, z_s, z_r,
-    y_s, y_r, yf_s, yf_r, ax_s, ax_r, az_s, az_r, bz_s, bz_r, bx_s, bx_r, m_s, m_r, out_s, out_r,
+    y_s, y_r, yf_s, yf_r, gx_s, gx_r, gz_s, gz_r, hz_s, hz_r, hx_s, hx_r,
+    ax_s, ax_r, az_s, az_r, bz_s, bz_r, bx_s, bx_r, m_s, m_r, out_s, out_r,
 ):
     y = lax.axis_index("y")
     zl = lax.axis_index("zl")
@@ -96,26 +97,34 @@
         t = xa.at[k, c, subs[j]]
         send(t, t, sib_s.at[k, j], sib_r.at[k, j], sibling)
 
-    def from_sibling(k):
-        for j in range(2):
-            arrived(xa.at[k, 1 - c, subs[j]], sib_s.at[k, j], sib_r.at[k, j])
-
-    def partial_margin(g):
-        off, n = GROUPS[g]
+    def from_sibling(k, j):
+        arrived(xa.at[k, 1 - c, subs[j]], sib_s.at[k, j], sib_r.at[k, j])
+
+    def partial_margin(g, j):
+        off, n = GROUPS[g]
+        s = subs[j]
         for p in range(off, off + n):
             k = SLOT[p]
-            for s in range(2):
-                v = dot(xa[k, 0, s], xa[0, 0, c], (((0,), (0,)), ((), ())))
-                v = v + dot(xa[k, 1, s], xa[0, 1, c], (((0,), (0,)), ((), ())))
-                v = v.astype(BF16)
-                xs[2 * s, p] = v[:xrows]
-                xs[2 * s + 1, p] = v[xrows:]
-        for d in range(1, NX):
-            dev = xdev(d)
-            send(
-                xs.at[dev["x"], pl.ds(off, n)], xr.at[d - 1, pl.ds(off, n)],
-                x_s.at[g, d - 1], x_r.at[g, d - 1], dev,
-            )
+            v = dot(xa[k, 0, s], xa[0, 0, c], (((0,), (0,)), ((), ())))
+            v = v + dot(xa[k, 1, s], xa[0, 1, c], (((0,), (0,)), ((), ())))
+            v = v.astype(BF16)
+            xs[2 * s, p] = v[:xrows]
+            xs[2 * s + 1, p] = v[xrows:]
+        for i in range(2):
+            to = 2 * s + i
+            d = lax.rem(to - x + NX, NX)
+            at = jnp.maximum(d - 1, 0)
+            h = copy(xs.at[to, pl.ds(off, n)], xr.at[at, pl.ds(off, n)], x_s.at[g, at], x_r.at[g, at], {"x": to})
+
+            @pl.when(d > 0)
+            def _():
+                h.start()
+
+    def partial_sent(g):
+        off, n = GROUPS[g]
+        for d in range(1, NX):
+            t = xr.at[d - 1, pl.ds(off, n)]
+            copy(t, t, x_s.at[g, d - 1], x_r.at[g, d - 1], sibling).wait_send()
 
     def sum_over_x(g):
         off, n = GROUPS[g]
@@ -147,7 +156,7 @@
             d32[p] = v
             w = v.astype(BF16)
             db[p] = w
-            put_own(da, dbb, p, w)
+            da[p, z, x] = w
 
     def unit(rows, cols, row0, col0):
         i = lax.broadcasted_iota(jnp.int32, (rows, cols), 0) + row0
@@ -166,33 +175,146 @@
         to_minus(0, j)
         to_plus(0, j)
         to_sibling(0, j)
-    for h in range(1, 5):
+    def ring_step(h, j):
+        if h < 4 or j == 0:
+            arrived(xa.at[h, c, subs[j]], ring_s.at[0, h - 1, j], ring_r.at[0, h - 1, j])
+            if h < 3 or (h == 3 and j == 0):
+                to_minus(h, j)
+            to_sibling(h, j)
+        if h < 4 or j == 1:
+            arrived(xa.at[NY - h, c, subs[j]], ring_s.at[1, h - 1, j], ring_r.at[1, h - 1, j])
+            if h < 3 or (h == 3 and j == 1):
+                to_plus(h, j)
+            to_sibling(NY - h, j)
+
+    def use(h, j):
+        if (h, j) == (1, 0):
+            from_sibling(0, 0)
+            from_sibling(0, 1)
+        from_sibling(h, j)
+        if h < 4:
+            from_sibling(NY - h, j)
+        partial_margin(h - 1, j)
+
+    def gather_x(g):
+        off, n = GROUPS[g]
+        v = da.at[pl.ds(off, n), z, x]
+        for d in range(1, NX):
+            send(v, v, gx_s.at[g, d - 1], gx_r.at[g, d - 1], xdev(d))
+
+    def slab(g, i, h):
+        off, n = GROUPS[g]
+        t = lax.rem(z + (h if i == 0 else NZ - h), NZ)
+        return t, pl.ds(off, n)
+
+    def hop_send(g, i, h):
+        t, ps = slab(g, i, h - 1)
+        v = da.at[ps, t] if h < 4 else da.at[ps, t, pl.ds(2 * i, 2)]
+        send(v, v, gz_s.at[g, i, h - 1], gz_r.at[g, i, h - 1], zdev(-1 if i == 0 else 1))
+
+    def gather_z(g):
+        off, n = GROUPS[g]
+        for d in range(1, NX):
+            t = lax.rem(x + NX - d, NX)
+            arrived(da.at[pl.ds(off, n), z, t], gx_s.at[g, d - 1], gx_r.at[g, d - 1])
+        for i in range(2):
+            hop_send(g, i, 1)
+
+    def hop(g, h):
+        for i in range(2):
+            t, ps = slab(g, i, h)
+            v = da.at[ps, t] if h < 4 else da.at[ps, t, pl.ds(2 * i, 2)]
+            arrived(v, gz_s.at[g, i, h - 1], gz_r.at[g, i, h - 1])
+            if h < 4:
+                hop_send(g, i, h + 1)
+
+    def near_z(g):
+        off, n = GROUPS[g]
+        v = da.at[pl.ds(off, n), z, x]
+        for d in range(1, NZ):
+            send(v, v, hz_s.at[g - 2, d - 1], hz_r.at[g - 2, d - 1], zdev(d))
+
+    def near_x(g):
+        off, n = GROUPS[g]
+        for d in range(1, NZ):
+            t = lax.rem(z + NZ - d, NZ)
+            arrived(da.at[pl.ds(off, n), t, x], hz_s.at[g - 2, d - 1], hz_r.at[g - 2, d - 1])
+        v = da.at[pl.ds(off, n), :, x]
+        for d in range(1, NX):
+            send(v, v, hx_s.at[g - 2, d - 1], hx_r.at[g - 2, d - 1], xdev(d))
+
+    def near_done(g):
+        off, n = GROUPS[g]
+        for d in range(1, NX):
+            t = lax.rem(x + NX - d, NX)
+            arrived(da.at[pl.ds(off, n), :, t], hx_s.at[g - 2, d - 1], hx_r.at[g - 2, d - 1])
+
+    PARTS = ((0, 5), (5, 3))
+
+    def rows_part(i):
+        off, n = PARTS[i]
+        return pl.ds(off, n)
+
+    def left_send(i):
+        ps = rows_part(i)
+        for k in range(1, NY):
+            send(db.at[ps], dj.at[k, c, ps], y_s.at[i, k - 1], y_r.at[i, k - 1], ydev(-k))
+        off, n = PARTS[i]
+        for p in range(off, off + n):
+            dj[0, c, p] = db[p]
+        if i == 1:
+            send(db, dj.at[0, c], yf_s.at[0], yf_r.at[0], sibling)
+
+    def left_pass():
+        for k in range(1, NY):
+            for i in range(2):
+                arrived(dj.at[k, c, rows_part(i)], y_s.at[i, k - 1], y_r.at[i, k - 1])
+            send(dj.at[k, c], dj.at[k, c], yf_s.at[k], yf_r.at[k], sibling)
+
+    for h in range(1, 4):
         for j in range(2):
-            if h < 4 or j == 0:
-                arrived(xa.at[h, c, subs[j]], ring_s.at[0, h - 1, j], ring_r.at[0, h - 1, j])
-                if h < 3 or (h == 3 and j == 0):
-                    to_minus(h, j)
-                to_sibling(h, j)
-            if h < 4 or j == 1:
-                arrived(xa.at[NY - h, c, subs[j]], ring_s.at[1, h - 1, j], ring_r.at[1, h - 1, j])
-                if h < 3 or (h == 3 and j == 1):
-                    to_plus(h, j)
-                to_sibling(NY - h, j)
-        if h == 1:
-            from_sibling(0)
-        from_sibling(h)
-        if h < 4:
-            from_sibling(NY - h)
-        partial_margin(h - 1)
-        if h > 1:
-            sum_over_x(h - 2)
-        if h > 2:
-            sum_over_z(h - 3)
+            ring_step(h, j)
+            use(h, j)
+            if (h, j) == (2, 1):
+                sum_over_x(0)
+            if (h, j) == (3, 0):
+                sum_over_x(1)
+            if (h, j) == (3, 1):
+                sum_over_z(0)
+                gather_x(0)
+    ring_step(4, 0)
+    ring_step(4, 1)
+    gather_z(0)
+    use(4, 0)
+    use(4, 1)
+    sum_over_x(2)
+    sum_over_z(1)
+    gather_x(1)
+    left_send(0)
+    hop(0, 1)
     sum_over_x(3)
+    gather_z(1)
     sum_over_z(2)
+    near_z(2)
+    hop(0, 2)
     sum_over_z(3)
-
-    def plane_gather(q, a, b, between, a_done):
+    near_z(3)
+    left_send(1)
+    hop(1, 1)
+    hop(0, 3)
+    hop(1, 2)
+    near_x(2)
+    hop(0, 4)
+    hop(1, 3)
+    near_x(3)
+    left_pass()
+    hop(1, 4)
+    near_done(2)
+    near_done(3)
+    for k in range(NY):
+        arrived(dj.at[k, 1 - c], yf_s.at[k], yf_r.at[k])
+
+    def plane_gather(a, b, between, a_done):
         def az(i, h):
             t = lax.rem(z + (h if i == 0 else NZ - h), NZ)
             if h < 4:
@@ -211,29 +333,29 @@
                 v = a.at[t] if h < 4 else a.at[t, pl.ds(2 * i, 2)]
             else:
                 v = b.at[x, t] if h < 4 else b.at[x, t, pl.ds(2 * i, 2)]
-            send(v, v, ss.at[q, i, h - 1], rs.at[q, i, h - 1], zdev(-1 if i == 0 else 1))
-
-        for d in range(1, NX):
-            send(a.at[z, x], a.at[z, x], ax_s.at[q, d - 1], ax_r.at[q, d - 1], xdev(d))
+            send(v, v, ss.at[i, h - 1], rs.at[i, h - 1], zdev(-1 if i == 0 else 1))
+
+        for d in range(1, NX):
+            send(a.at[z, x], a.at[z, x], ax_s.at[d - 1], ax_r.at[d - 1], xdev(d))
         for i in range(2):
             ring(1, i, 1, bz_s, bz_r)
 
         def b_hop(h):
             for i in range(2):
-                arrived(bz(i, h), bz_s.at[q, i, h - 1], bz_r.at[q, i, h - 1])
+                arrived(bz(i, h), bz_s.at[i, h - 1], bz_r.at[i, h - 1])
                 if h < 4:
                     ring(1, i, h + 1, bz_s, bz_r)
 
         def a_hop(h):
             for i in range(2):
-                arrived(az(i, h), az_s.at[q, i, h - 1], az_r.at[q, i, h - 1])
+                arrived(az(i, h), az_s.at[i, h - 1], az_r.at[i, h - 1])
                 if h < 4:
                     ring(0, i, h + 1, az_s, az_r)
 
         b_hop(1)
         for d in range(1, NX):
             t = lax.rem(x + NX - d, NX)
-            arrived(a.at[z, t], ax_s.at[q, d - 1], ax_r.at[q, d - 1])
+            arrived(a.at[z, t], ax_s.at[d - 1], ax_r.at[d - 1])
         for i in range(2):
             ring(0, i, 1, az_s, az_r)
         b_hop(2)
@@ -241,34 +363,20 @@
         a_hop(1)
         b_hop(4)
         for i in range(2):
-            send(b.at[x], b.at[x], bx_s.at[q, i, 0], bx_r.at[q, i, 0], xdev(-1 if i == 0 else 1))
+            send(b.at[x], b.at[x], bx_s.at[i, 0], bx_r.at[i, 0], xdev(-1 if i == 0 else 1))
         between()
         a_hop(2)
         a_hop(3)
         for i in range(2):
             t = lax.rem(x + (1 if i == 0 else NX - 1), NX)
-            arrived(b.at[t], bx_s.at[q, i, 0], bx_r.at[q, i, 0])
+            arrived(b.at[t], bx_s.at[i, 0], bx_r.at[i, 0])
             v = b.at[t, pl.ds(4 * i, 4)]
-            send(v, v, bx_s.at[q, i, 1], bx_r.at[q, i, 1], xdev(-1 if i == 0 else 1))
+            send(v, v, bx_s.at[i, 1], bx_r.at[i, 1], xdev(-1 if i == 0 else 1))
         a_hop(4)
         a_done()
         for i in range(2):
             t = lax.rem(x + 2, NX)
-            arrived(b.at[t, pl.ds(4 * i, 4)], bx_s.at[q, i, 1], bx_r.at[q, i, 1])
-
-    dj[0, c] = db[...].reshape(NY * zrows, band)
-    send(dj.at[0, c], dj.at[0, c], yf_s.at[0], yf_r.at[0], sibling)
-    for k in range(1, NY):
-        send(dj.at[0, c], dj.at[k, c], y_s.at[k - 1], y_r.at[k - 1], ydev(-k))
-
-    def pass_on():
-        for k in range(1, NY):
-            arrived(dj.at[k, c], y_s.at[k - 1], y_r.at[k - 1])
-            send(dj.at[k, c], dj.at[k, c], yf_s.at[k], yf_r.at[k], sibling)
-
-    plane_gather(0, da, dbb, pass_on, lambda: None)
-    for k in range(NY):
-        arrived(dj.at[k, 1 - c], yf_s.at[k], yf_r.at[k])
+            arrived(b.at[t, pl.ds(4 * i, 4)], bx_s.at[i, 1], bx_r.at[i, 1])
 
     def quarter(a, b, p, q):
         v = a[:, q, p] if p < 4 else b[q, :, p - 4]
@@ -277,9 +385,13 @@
     def rows_of(a, b, p, s):
         return jnp.concatenate([quarter(a, b, p, 2 * s), quarter(a, b, p, 2 * s + 1)], axis=0)
 
+    def dev_rows(p, s):
+        return jnp.concatenate([da[p, :, 2 * s + i].reshape(xrows, band) for i in range(2)], axis=0)
+
     acc_sq = [None] * NY
     for k in range(NY):
-        part = dot(dj[k, 0], rows_of(da, dbb, POS[k], 0)) + dot(dj[k, 1], rows_of(da, dbb, POS[k], 1))
+        left = [dj[k, s].reshape(NY * zrows, band) for s in range(2)]
+        part = dot(left[0], dev_rows(POS[k], 0)) + dot(left[1], dev_rows(POS[k], 1))
         for p in range(NY):
             m = POS[(k + SLOT[p]) % NY]
             piece = part[p * zrows : (p + 1) * zrows]
@@ -292,14 +404,10 @@
 
     kg = lax.rem(x * 2 + zh // 2 - y + NY, NY)
     pg = jnp.where(kg == 0, 0, jnp.where(kg <= 4, 2 * kg - 1, 2 * (NY - kg)))
-    pa = jnp.minimum(pg, 3)
-    pb = jnp.maximum(pg - 4, 0)
 
     def mirror(core):
         q = lax.rem(zh, 2) * 2 + core
-        va = da[:, q, pa].reshape(xrows, band)
-        vb = dbb[q, :, pb].reshape(xrows, band)
-        return jnp.where(pg < 4, va.astype(F32), vb.astype(F32))
+        return da[pg, :, q].reshape(xrows, band).astype(F32)
 
     def margin_work():
         ms[...] = mirror(1 - c).astype(BF16)
@@ -338,7 +446,7 @@
         m_out[...] = v.T + unit(band, xrows, rows0, cols0)
         product(0)
 
-    plane_gather(1, ca, cbb, margin_work, first_half)
+    plane_gather(ca, cbb, margin_work, first_half)
     product(1)
 
     other = o_out.at[pl.ds((1 - zl) * half, half), :]
@@ -356,6 +464,8 @@
                 osb.at[cc], o_out.at[pl.ds(zl * half, half), :], out_s.at[cc], out_r.at[zl], {"zl": c, "c": cc}
             ).wait_send()
 
+    for g in range(len(GROUPS)):
+        partial_sent(g)
     for h in sends:
         h.wait_send()
 
@@ -376,10 +486,8 @@
         v((NZ - 1, NY, zrows, band), BF16),
         v((NY, zrows, band), BF16),
         v((NY, zrows, band), F32),
-        v((NY, 2, NY * zrows, band), BF16),
-        v((NZ, NX, 4, zrows, band), BF16),
-        v((NX, NZ, 4, zrows, band), BF16),
-        v((NY, zrows, band), BF16),
+        v((NY, 2, NY, zrows, band), BF16),
+        v((NY, NZ, NX, zrows, band), BF16),
         v((NZ, NX, 4, zrows, band), BF16),
         v((NX, NZ, 4, zrows, band), BF16),
         v((xrows, band), BF16),
@@ -392,12 +500,16 @@
         dma((NY, 2)), dma((NY, 2)),
         dma((4, NX - 1)), dma((4, NX - 1)),
         dma((4, NZ - 1)), dma((4, NZ - 1)),
-        dma((NY - 1,)), dma((NY - 1,)),
+        dma((2, NY - 1)), dma((2, NY - 1)),
         dma((NY,)), dma((NY,)),
         dma((2, NX - 1)), dma((2, NX - 1)),
         dma((2, 2, 4)), dma((2, 2, 4)),
-        dma((2, 2, 4)), dma((2, 2, 4)),
-        dma((2, 2, 2)), dma((2, 2, 2)),
+        dma((2, NZ - 1)), dma((2, NZ - 1)),
+        dma((2, NX - 1)), dma((2, NX - 1)),
+        dma((NX - 1,)), dma((NX - 1,)),
+        dma((2, 4)), dma((2, 4)),
+        dma((2, 4)), dma((2, 4)),
+        dma((2, 2)), dma((2, 2)),
         dma, dma,
         dma((2,)), dma((2,)),
     ]

time: 139 us -> 137 us (0.986)
  Pallas kernels: 135 us -> 133 us
    pallas_call x1, Pallas kernels: 135 us -> 133 us  [shards(): pl.pallas_call(body, out_shape=(jax.ShapeDtypeStruct((band, xrows), F32),...]
where the time goes in v2:
time: 137 us
  Pallas kernels  133 us (97%)
  local copies, waits for them, and re-layouts  3.44 us (3%)
    pallas_call x1, Pallas kernels, shards(): pl.pallas_call(body, out_shape=(jax.ShapeDtypeStruct((band, xrows), F32),...  133 us
    unnamed x2, local copies, waits for them, and re-layouts  3.44 us

profile of v2, /device:TPU:1, one launch (start us, length us, event | category | flops | bytes accessed | tf_op | source)
XLA Modules:
  0.0 137.1 jit_solution(8551873814157506831)
XLA Ops:
  0.6 133.0 %shard_map.30 = (f32[256,128]{1,0:T(8,128)}, bf16[1024,256]{1,0:T(8,128)(2,1)}) custom-call(bf16[1024,256]{1,0:T(8,128)(2,1)} %refs_0_.1), custom_call_target="tpu_custom_call" | custom-call | tf_op jit(solution)/shard_map/pallas_call | solution.py:520
  133.6 1.6 %copy.5 = f32[256,128]{1,0:T(8,128)} copy(f32[256,128]{1,0:T(8,128)} %get-tuple-element.4) | data formatting | bytes 262144
  135.2 1.9 %copy.6 = bf16[1024,256]{1,0:T(8,128)(2,1)} copy(bf16[1024,256]{1,0:T(8,128)(2,1)} %get-tuple-element.5) | data formatting | bytes 1048576

commit v3 on v2

--- a/solution.py
+++ b/solution.py
@@ -21,7 +21,7 @@
 
 
 def kernel(
-    total_rows, x_hbm, m_out, o_out, xa, ph, xs, xr, zs, zr, db, d32, dj, da, ca, cbb,
+    total_rows, x_hbm, m_out, o_out, xa, ph, xs, xr, zs, zr, db, d32, dj, da, ca,
     ms, mr, acc, osb, in_sem, sw_s, sw_r, ring_s, ring_r, sib_s, sib_r, x_s, x_r, z_s, z_r,
     y_s, y_r, yf_s, yf_r, gx_s, gx_r, gz_s, gz_r, hz_s, hz_r, hx_s, hx_r,
     ax_s, ax_r, az_s, az_r, bz_s, bz_r, bx_s, bx_r, m_s, m_r, out_s, out_r,
@@ -162,12 +162,6 @@
         i = lax.broadcasted_iota(jnp.int32, (rows, cols), 0) + row0
         j = lax.broadcasted_iota(jnp.int32, (rows, cols), 1) + col0
         return (i == j).astype(F32)
-
-    def put_own(a, b, p, w):
-        if p < 4:
-            a[z, x, p] = w
-        else:
-            b[x, z, p - 4] = w
 
     for j in range(2):
         if j == 1:
@@ -232,22 +226,22 @@
         off, n = GROUPS[g]
         v = da.at[pl.ds(off, n), z, x]
         for d in range(1, NZ):
-            send(v, v, hz_s.at[g - 2, d - 1], hz_r.at[g - 2, d - 1], zdev(d))
+            send(v, v, hz_s.at[g - 1, d - 1], hz_r.at[g - 1, d - 1], zdev(d))
 
     def near_x(g):
         off, n = GROUPS[g]
         for d in range(1, NZ):
             t = lax.rem(z + NZ - d, NZ)
-            arrived(da.at[pl.ds(off, n), t, x], hz_s.at[g - 2, d - 1], hz_r.at[g - 2, d - 1])
+            arrived(da.at[pl.ds(off, n), t, x], hz_s.at[g - 1, d - 1], hz_r.at[g - 1, d - 1])
         v = da.at[pl.ds(off, n), :, x]
         for d in range(1, NX):
-            send(v, v, hx_s.at[g - 2, d - 1], hx_r.at[g - 2, d - 1], xdev(d))
+            send(v, v, hx_s.at[g - 1, d - 1], hx_r.at[g - 1, d - 1], xdev(d))
 
     def near_done(g):
         off, n = GROUPS[g]
         for d in range(1, NX):
             t = lax.rem(x + NX - d, NX)
-            arrived(da.at[pl.ds(off, n), :, t], hx_s.at[g - 2, d - 1], hx_r.at[g - 2, d - 1])
+            arrived(da.at[pl.ds(off, n), :, t], hx_s.at[g - 1, d - 1], hx_r.at[g - 1, d - 1])
 
     PARTS = ((0, 5), (5, 3))
 
@@ -274,116 +268,110 @@
     for h in range(1, 4):
         for j in range(2):
             ring_step(h, j)
+            if (h, j) == (3, 0):
+                sum_over_z(0)
+                gather_x(0)
             use(h, j)
-            if (h, j) == (2, 1):
+            if (h, j) == (2, 0):
                 sum_over_x(0)
             if (h, j) == (3, 0):
                 sum_over_x(1)
-            if (h, j) == (3, 1):
-                sum_over_z(0)
-                gather_x(0)
+                gather_z(0)
+    hop(0, 1)
     ring_step(4, 0)
     ring_step(4, 1)
-    gather_z(0)
+    sum_over_z(1)
+    near_z(1)
+    hop(0, 2)
     use(4, 0)
     use(4, 1)
     sum_over_x(2)
-    sum_over_z(1)
-    gather_x(1)
     left_send(0)
-    hop(0, 1)
+    hop(0, 3)
+    near_x(1)
     sum_over_x(3)
-    gather_z(1)
     sum_over_z(2)
     near_z(2)
-    hop(0, 2)
     sum_over_z(3)
     near_z(3)
     left_send(1)
-    hop(1, 1)
-    hop(0, 3)
-    hop(1, 2)
     near_x(2)
+    near_x(3)
     hop(0, 4)
-    hop(1, 3)
-    near_x(3)
     left_pass()
-    hop(1, 4)
+    near_done(1)
     near_done(2)
     near_done(3)
     for k in range(NY):
         arrived(dj.at[k, 1 - c], yf_s.at[k], yf_r.at[k])
 
-    def plane_gather(a, b, between, a_done):
-        def az(i, h):
-            t = lax.rem(z + (h if i == 0 else NZ - h), NZ)
+    def piece(b, t, u):
+        return ca.at[t, u, pl.ds(4 * b, 4)]
+
+    def zpiece(b, u, i, h, far):
+        t = lax.rem(z + (h if i == 0 else NZ - h), NZ)
+        return ca.at[t, u, pl.ds(4 * b + 2 * i, 2)] if far else piece(b, t, u)
+
+    def a_send(d, i, h):
+        v = zpiece(0, lax.rem(x + NX - d, NX), i, h - 1, h == 4)
+        send(v, v, az_s.at[d, i, h - 1], az_r.at[d, i, h - 1], zdev(-1 if i == 0 else 1))
+
+    def a_hop(d, h):
+        for i in range(2):
+            v = zpiece(0, lax.rem(x + NX - d, NX), i, h, h == 4)
+            arrived(v, az_s.at[d, i, h - 1], az_r.at[d, i, h - 1])
             if h < 4:
-                return a.at[t]
-            return a.at[t, pl.ds(2 * i, 2)]
-
-        def bz(i, h):
-            t = lax.rem(z + (h if i == 0 else NZ - h), NZ)
+                a_send(d, i, h + 1)
+
+    def b_send(i, h):
+        v = zpiece(1, x, i, h - 1, h == 4)
+        send(v, v, bz_s.at[i, h - 1], bz_r.at[i, h - 1], zdev(-1 if i == 0 else 1))
+
+    def b_along_x(r):
+        v = piece(1, lax.rem(z + r, NZ), x)
+        for d in (1, 3, 2):
+            send(v, v, bx_s.at[r, d - 1], bx_r.at[r, d - 1], xdev(d))
+
+    def b_hop(h):
+        for i in range(2):
+            arrived(zpiece(1, x, i, h, h == 4), bz_s.at[i, h - 1], bz_r.at[i, h - 1])
             if h < 4:
-                return b.at[x, t]
-            return b.at[x, t, pl.ds(2 * i, 2)]
-
-        def ring(blk, i, h, ss, rs):
-            t = lax.rem(z + (h - 1 if i == 0 else NZ - h + 1), NZ)
-            if blk == 0:
-                v = a.at[t] if h < 4 else a.at[t, pl.ds(2 * i, 2)]
-            else:
-                v = b.at[x, t] if h < 4 else b.at[x, t, pl.ds(2 * i, 2)]
-            send(v, v, ss.at[i, h - 1], rs.at[i, h - 1], zdev(-1 if i == 0 else 1))
-
-        for d in range(1, NX):
-            send(a.at[z, x], a.at[z, x], ax_s.at[d - 1], ax_r.at[d - 1], xdev(d))
-        for i in range(2):
-            ring(1, i, 1, bz_s, bz_r)
-
-        def b_hop(h):
+                b_send(i, h + 1)
+        if h < 4:
+            b_along_x(h)
+            b_along_x(NZ - h)
+        else:
+            b_along_x(4)
+
+    def plane_gather(between, a_done):
+        for d in (1, 3, 2):
+            send(piece(0, z, x), piece(0, z, x), ax_s.at[d - 1], ax_r.at[d - 1], xdev(d))
+        for i in range(2):
+            b_send(i, 1)
+        for i in range(2):
+            a_send(0, i, 1)
+        b_along_x(0)
+        b_hop(1)
+        for d in (1, 3, 2):
+            u = lax.rem(x + NX - d, NX)
+            arrived(piece(0, z, u), ax_s.at[d - 1], ax_r.at[d - 1])
             for i in range(2):
-                arrived(bz(i, h), bz_s.at[i, h - 1], bz_r.at[i, h - 1])
-                if h < 4:
-                    ring(1, i, h + 1, bz_s, bz_r)
-
-        def a_hop(h):
-            for i in range(2):
-                arrived(az(i, h), az_s.at[i, h - 1], az_r.at[i, h - 1])
-                if h < 4:
-                    ring(0, i, h + 1, az_s, az_r)
-
-        b_hop(1)
-        for d in range(1, NX):
-            t = lax.rem(x + NX - d, NX)
-            arrived(a.at[z, t], ax_s.at[d - 1], ax_r.at[d - 1])
-        for i in range(2):
-            ring(0, i, 1, az_s, az_r)
-        b_hop(2)
-        b_hop(3)
-        a_hop(1)
-        b_hop(4)
-        for i in range(2):
-            send(b.at[x], b.at[x], bx_s.at[i, 0], bx_r.at[i, 0], xdev(-1 if i == 0 else 1))
+                a_send(d, i, 1)
+        a_hop(0, 1)
         between()
-        a_hop(2)
-        a_hop(3)
-        for i in range(2):
-            t = lax.rem(x + (1 if i == 0 else NX - 1), NX)
-            arrived(b.at[t], bx_s.at[i, 0], bx_r.at[i, 0])
-            v = b.at[t, pl.ds(4 * i, 4)]
-            send(v, v, bx_s.at[i, 1], bx_r.at[i, 1], xdev(-1 if i == 0 else 1))
-        a_hop(4)
+        for h in range(2, 6):
+            if h < 5:
+                b_hop(h)
+                a_hop(0, h)
+            for d in (1, 3, 2):
+                a_hop(d, h - 1)
         a_done()
-        for i in range(2):
-            t = lax.rem(x + 2, NX)
-            arrived(b.at[t, pl.ds(4 * i, 4)], bx_s.at[i, 1], bx_r.at[i, 1])
-
-    def quarter(a, b, p, q):
-        v = a[:, q, p] if p < 4 else b[q, :, p - 4]
-        return v.reshape(xrows, band)
-
-    def rows_of(a, b, p, s):
-        return jnp.concatenate([quarter(a, b, p, 2 * s), quarter(a, b, p, 2 * s + 1)], axis=0)
+        for r in (0, 1, 7, 2, 6, 3, 5, 4):
+            for d in (1, 3, 2):
+                arrived(piece(1, lax.rem(z + r, NZ), lax.rem(x + NX - d, NX)), bx_s.at[r, d - 1], bx_r.at[r, d - 1])
+
+    def rows_of(p, s):
+        return jnp.concatenate([ca[:, 2 * s + i, p].reshape(xrows, band) for i in range(2)], axis=0)
 
     def dev_rows(p, s):
         return jnp.concatenate([da[p, :, 2 * s + i].reshape(xrows, band) for i in range(2)], axis=0)
@@ -394,13 +382,13 @@
         part = dot(left[0], dev_rows(POS[k], 0)) + dot(left[1], dev_rows(POS[k], 1))
         for p in range(NY):
             m = POS[(k + SLOT[p]) % NY]
-            piece = part[p * zrows : (p + 1) * zrows]
-            acc_sq[m] = piece if acc_sq[m] is None else acc_sq[m] + piece
+            rows = part[p * zrows : (p + 1) * zrows]
+            acc_sq[m] = rows if acc_sq[m] is None else acc_sq[m] + rows
     for p in range(NY):
         v = 0.375 * acc_sq[p] - 0.5 * d32[p]
         if p == 0:
             v = v + unit(zrows, band, x * xrows + z * zrows, c * band)
-        put_own(ca, cbb, p, v.astype(BF16))
+        ca[z, x, p] = v.astype(BF16)
 
     kg = lax.rem(x * 2 + zh // 2 - y + NY, NY)
     pg = jnp.where(kg == 0, 0, jnp.where(kg <= 4, 2 * kg - 1, 2 * (NY - kg)))
@@ -418,7 +406,7 @@
             for p in range(4 * part, 4 * part + 4):
                 k = SLOT[p]
                 for s in range(2):
-                    v = dot(xa[k, cc, s], rows_of(ca, cbb, p, s))
+                    v = dot(xa[k, cc, s], rows_of(p, s))
                     if part == 0 and p == 0 and s == 0:
                         acc[cc] = v
                     else:
@@ -446,7 +434,7 @@
         m_out[...] = v.T + unit(band, xrows, rows0, cols0)
         product(0)
 
-    plane_gather(ca, cbb, margin_work, first_half)
+    plane_gather(margin_work, first_half)
     product(1)
 
     other = o_out.at[pl.ds((1 - zl) * half, half), :]
@@ -488,8 +476,7 @@
         v((NY, zrows, band), F32),
         v((NY, 2, NY, zrows, band), BF16),
         v((NY, NZ, NX, zrows, band), BF16),
-        v((NZ, NX, 4, zrows, band), BF16),
-        v((NX, NZ, 4, zrows, band), BF16),
+        v((NZ, NX, NY, zrows, band), BF16),
         v((xrows, band), BF16),
         v((xrows, band), BF16),
         v((2, half, band), F32),
@@ -502,14 +489,14 @@
         dma((4, NZ - 1)), dma((4, NZ - 1)),
         dma((2, NY - 1)), dma((2, NY - 1)),
         dma((NY,)), dma((NY,)),
-        dma((2, NX - 1)), dma((2, NX - 1)),
-        dma((2, 2, 4)), dma((2, 2, 4)),
-        dma((2, NZ - 1)), dma((2, NZ - 1)),
-        dma((2, NX - 1)), dma((2, NX - 1)),
+        dma((1, NX - 1)), dma((1, NX - 1)),
+        dma((1, 2, 4)), dma((1, 2, 4)),
+        dma((3, NZ - 1)), dma((3, NZ - 1)),
+        dma((3, NX - 1)), dma((3, NX - 1)),
         dma((NX - 1,)), dma((NX - 1,)),
+        dma((NX, 2, 4)), dma((NX, 2, 4)),
         dma((2, 4)), dma((2, 4)),
-        dma((2, 4)), dma((2, 4)),
-        dma((2, 2)), dma((2, 2)),
+        dma((NZ, NX - 1)), dma((NZ, NX - 1)),
         dma, dma,
         dma((2,)), dma((2,)),
     ]

time: 137 us -> 130 us (0.949); the launches traced: 137 us -> 128 us
  Pallas kernels: 133 us -> 124 us
    pallas_call x1, Pallas kernels: 133 us -> 124 us  [shards(): pl.pallas_call(body, out_shape=(jax.ShapeDtypeStruct((band, xrows), F32),...]
where the time goes in v3:
time: 130 us; the launch traced here: 128 us
  Pallas kernels  124 us (95%)
  local copies, waits for them, and re-layouts  3.44 us (3%)
    pallas_call x1, Pallas kernels, shards(): pl.pallas_call(body, out_shape=(jax.ShapeDtypeStruct((band, xrows), F32),...  124 us
    unnamed x2, local copies, waits for them, and re-layouts  3.44 us

profile of v3, /device:TPU:1, one launch (start us, length us, event | category | flops | bytes accessed | tf_op | source)
XLA Modules:
  0.0 128.5 jit_solution(15538576004287334937)
XLA Ops:
  0.6 124.4 %shard_map.30 = (f32[256,128]{1,0:T(8,128)}, bf16[1024,256]{1,0:T(8,128)(2,1)}) custom-call(bf16[1024,256]{1,0:T(8,128)(2,1)} %refs_0_.1), custom_call_target="tpu_custom_call" | custom-call | tf_op jit(solution)/shard_map/pallas_call | solution.py:507
  125.0 1.6 %copy.5 = f32[256,128]{1,0:T(8,128)} copy(f32[256,128]{1,0:T(8,128)} %get-tuple-element.4) | data formatting | bytes 262144
  126.6 1.9 %copy.6 = bf16[1024,256]{1,0:T(8,128)(2,1)} copy(bf16[1024,256]{1,0:T(8,128)(2,1)} %get-tuple-element.5) | data formatting | bytes 1048576

commit v4 on v3

--- a/solution.py
+++ b/solution.py
@@ -8,9 +8,11 @@
 
 AXES = ("y", "zl", "x", "zh", "c")
 NY, NX, NZ = 8, 4, 8
-SLOT = (0, 1, 7, 2, 6, 3, 5, 4)
+SLOT = (0, 1, 7, 2, 6, 4, 3, 5)
 POS = tuple(SLOT.index(k) for k in range(NY))
-GROUPS = ((0, 3), (3, 2), (5, 2), (7, 1))
+GROUPS = ((0, 3), (3, 2), (6, 2), (5, 1))
+FACTORS = ((0, 0), (1, 0), (7, 0), (2, 0), (6, 0), (2, 6), (3, 0), (5, 0))
+FAR = 5
 MESH_ID = pl.DeviceIdType.MESH
 F32 = jnp.float32
 BF16 = jnp.bfloat16
@@ -21,9 +23,9 @@
 
 
 def kernel(
-    total_rows, x_hbm, m_out, o_out, xa, ph, xs, xr, zs, zr, db, d32, dj, da, ca,
+    total_rows, x_hbm, m_out, o_out, xa, ph, xs, xr, zs, zr, db, d32, dq, dj, da, ca,
     ms, mr, acc, osb, in_sem, sw_s, sw_r, ring_s, ring_r, sib_s, sib_r, x_s, x_r, z_s, z_r,
-    y_s, y_r, yf_s, yf_r, gx_s, gx_r, gz_s, gz_r, hz_s, hz_r, hx_s, hx_r,
+    q_s, q_r, y_s, y_r, yf_s, yf_r, gx_s, gx_r, gz_s, gz_r, hz_s, hz_r, hx_s, hx_r,
     ax_s, ax_r, az_s, az_r, bz_s, bz_r, bx_s, bx_r, m_s, m_r, out_s, out_r,
 ):
     y = lax.axis_index("y")
@@ -104,9 +106,9 @@
         off, n = GROUPS[g]
         s = subs[j]
         for p in range(off, off + n):
-            k = SLOT[p]
-            v = dot(xa[k, 0, s], xa[0, 0, c], (((0,), (0,)), ((), ())))
-            v = v + dot(xa[k, 1, s], xa[0, 1, c], (((0,), (0,)), ((), ())))
+            k, r = FACTORS[p]
+            v = dot(xa[k, 0, s], xa[r, 0, c], (((0,), (0,)), ((), ())))
+            v = v + dot(xa[k, 1, s], xa[r, 1, c], (((0,), (0,)), ((), ())))
             v = v.astype(BF16)
             xs[2 * s, p] = v[:xrows]
             xs[2 * s + 1, p] = v[xrows:]
@@ -153,10 +155,18 @@
             v = v * (1.0 / total_rows)
             if p == 0:
                 v = v - unit(zrows, band, x * xrows + z * zrows, c * band)
-            d32[p] = v
             w = v.astype(BF16)
-            db[p] = w
-            da[p, z, x] = w
+            if p == FAR:
+                dq[...] = w
+                send(dq, db.at[p], q_s, q_r, ydev(-2))
+            else:
+                d32[p] = v
+                db[p] = w
+                da[p, z, x] = w
+
+    def place_far():
+        arrived(db.at[FAR], q_s, q_r)
+        da[FAR, z, x] = db[FAR]
 
     def unit(rows, cols, row0, col0):
         i = lax.broadcasted_iota(jnp.int32, (rows, cols), 0) + row0
@@ -181,15 +191,6 @@
                 to_plus(h, j)
             to_sibling(NY - h, j)
 
-    def use(h, j):
-        if (h, j) == (1, 0):
-            from_sibling(0, 0)
-            from_sibling(0, 1)
-        from_sibling(h, j)
-        if h < 4:
-            from_sibling(NY - h, j)
-        partial_margin(h - 1, j)
-
     def gather_x(g):
         off, n = GROUPS[g]
         v = da.at[pl.ds(off, n), z, x]
@@ -226,7 +227,7 @@
         off, n = GROUPS[g]
         v = da.at[pl.ds(off, n), z, x]
         for d in range(1, NZ):
-            send(v, v, hz_s.at[g - 1, d - 1], hz_r.at[g - 1, d - 1], zdev(d))
+            send(db.at[pl.ds(off, n)], v, hz_s.at[g - 1, d - 1], hz_r.at[g - 1, d - 1], zdev(d))
 
     def near_x(g):
         off, n = GROUPS[g]
@@ -243,7 +244,7 @@
             t = lax.rem(x + NX - d, NX)
             arrived(da.at[pl.ds(off, n), :, t], hx_s.at[g - 1, d - 1], hx_r.at[g - 1, d - 1])
 
-    PARTS = ((0, 5), (5, 3))
+    PARTS = ((0, 6), (6, 2))
 
     def rows_part(i):
         off, n = PARTS[i]
@@ -265,43 +266,61 @@
                 arrived(dj.at[k, c, rows_part(i)], y_s.at[i, k - 1], y_r.at[i, k - 1])
             send(dj.at[k, c], dj.at[k, c], yf_s.at[k], yf_r.at[k], sibling)
 
-    for h in range(1, 4):
-        for j in range(2):
-            ring_step(h, j)
-            if (h, j) == (3, 0):
-                sum_over_z(0)
-                gather_x(0)
-            use(h, j)
-            if (h, j) == (2, 0):
-                sum_over_x(0)
-            if (h, j) == (3, 0):
-                sum_over_x(1)
-                gather_z(0)
+    def pair_in(h, j):
+        from_sibling(h, j)
+        from_sibling(NY - h, j)
+
+    ring_step(1, 0)
+    from_sibling(0, 0)
+    from_sibling(0, 1)
+    pair_in(1, 0)
+    partial_margin(0, 0)
+    ring_step(1, 1)
+    pair_in(1, 1)
+    partial_margin(0, 1)
+    ring_step(2, 0)
+    pair_in(2, 0)
+    partial_margin(1, 0)
+    sum_over_x(0)
+    ring_step(2, 1)
+    pair_in(2, 1)
+    partial_margin(3, 0)
+    partial_margin(3, 1)
+    partial_margin(1, 1)
+    ring_step(3, 0)
+    sum_over_z(0)
+    gather_x(0)
+    pair_in(3, 0)
+    partial_margin(2, 0)
+    sum_over_x(3)
+    sum_over_x(1)
+    gather_z(0)
+    ring_step(3, 1)
+    pair_in(3, 1)
+    partial_margin(2, 1)
+    sum_over_z(3)
+    sum_over_z(1)
+    near_z(1)
     hop(0, 1)
+    sum_over_x(2)
+    place_far()
+    near_z(3)
+    left_send(0)
     ring_step(4, 0)
     ring_step(4, 1)
-    sum_over_z(1)
-    near_z(1)
     hop(0, 2)
-    use(4, 0)
-    use(4, 1)
-    sum_over_x(2)
-    left_send(0)
-    hop(0, 3)
     near_x(1)
-    sum_over_x(3)
     sum_over_z(2)
     near_z(2)
-    sum_over_z(3)
-    near_z(3)
     left_send(1)
+    near_x(3)
+    hop(0, 3)
     near_x(2)
-    near_x(3)
     hop(0, 4)
     left_pass()
     near_done(1)
+    near_done(3)
     near_done(2)
-    near_done(3)
     for k in range(NY):
         arrived(dj.at[k, 1 - c], yf_s.at[k], yf_r.at[k])
 
@@ -343,7 +362,7 @@
         else:
             b_along_x(4)
 
-    def plane_gather(between, a_done):
+    def plane_gather(between, b_done):
         for d in (1, 3, 2):
             send(piece(0, z, x), piece(0, z, x), ax_s.at[d - 1], ax_r.at[d - 1], xdev(d))
         for i in range(2):
@@ -363,12 +382,14 @@
             if h < 5:
                 b_hop(h)
                 a_hop(0, h)
+            else:
+                for r in (0, 1, 7, 2, 6, 3, 5, 4):
+                    for d in (1, 3, 2):
+                        v = piece(1, lax.rem(z + r, NZ), lax.rem(x + NX - d, NX))
+                        arrived(v, bx_s.at[r, d - 1], bx_r.at[r, d - 1])
+                b_done()
             for d in (1, 3, 2):
                 a_hop(d, h - 1)
-        a_done()
-        for r in (0, 1, 7, 2, 6, 3, 5, 4):
-            for d in (1, 3, 2):
-                arrived(piece(1, lax.rem(z + r, NZ), lax.rem(x + NX - d, NX)), bx_s.at[r, d - 1], bx_r.at[r, d - 1])
 
     def rows_of(p, s):
         return jnp.concatenate([ca[:, 2 * s + i, p].reshape(xrows, band) for i in range(2)], axis=0)
@@ -385,19 +406,22 @@
             rows = part[p * zrows : (p + 1) * zrows]
             acc_sq[m] = rows if acc_sq[m] is None else acc_sq[m] + rows
     for p in range(NY):
-        v = 0.375 * acc_sq[p] - 0.5 * d32[p]
+        v = 0.375 * acc_sq[p] - 0.5 * (db[p].astype(F32) if p == FAR else d32[p])
         if p == 0:
             v = v + unit(zrows, band, x * xrows + z * zrows, c * band)
         ca[z, x, p] = v.astype(BF16)
 
     kg = lax.rem(x * 2 + zh // 2 - y + NY, NY)
-    pg = jnp.where(kg == 0, 0, jnp.where(kg <= 4, 2 * kg - 1, 2 * (NY - kg)))
+    near = jnp.where(kg == 0, 0, jnp.where(kg <= 2, 2 * kg - 1, 2 * (NY - kg)))
+    pg = jnp.where(kg == 3, 6, jnp.where(kg == 4, FAR, jnp.where(kg == 5, 7, near)))
 
     def mirror(core):
         q = lax.rem(zh, 2) * 2 + core
         return da[pg, :, q].reshape(xrows, band).astype(F32)
 
     def margin_work():
+        from_sibling(4, 0)
+        from_sibling(4, 1)
         ms[...] = mirror(1 - c).astype(BF16)
         send(ms, mr, m_s, m_r, sibling)
 
@@ -407,11 +431,11 @@
                 k = SLOT[p]
                 for s in range(2):
                     v = dot(xa[k, cc, s], rows_of(p, s))
-                    if part == 0 and p == 0 and s == 0:
+                    if part == 1 and p == 4 and s == 0:
                         acc[cc] = v
                     else:
                         acc[cc] += v
-            if part == 1:
+            if part == 0:
                 osb[cc] = acc[cc].astype(BF16)
                 mine = (zl == c) & (c == cc)
                 to = copy(
@@ -432,10 +456,10 @@
         rows0 = (y * 2 + zl) * band
         cols0 = (x * 8 + zh * 2 + c) * xrows
         m_out[...] = v.T + unit(band, xrows, rows0, cols0)
-        product(0)
+        product(1)
 
     plane_gather(margin_work, first_half)
-    product(1)
+    product(0)
 
     other = o_out.at[pl.ds((1 - zl) * half, half), :]
     arrived(other, out_s.at[0], out_r.at[1 - zl])
@@ -474,6 +498,7 @@
         v((NZ - 1, NY, zrows, band), BF16),
         v((NY, zrows, band), BF16),
         v((NY, zrows, band), F32),
+        v((zrows, band), BF16),
         v((NY, 2, NY, zrows, band), BF16),
         v((NY, NZ, NX, zrows, band), BF16),
         v((NZ, NX, NY, zrows, band), BF16),
@@ -487,6 +512,7 @@
         dma((NY, 2)), dma((NY, 2)),
         dma((4, NX - 1)), dma((4, NX - 1)),
         dma((4, NZ - 1)), dma((4, NZ - 1)),
+        dma, dma,
         dma((2, NY - 1)), dma((2, NY - 1)),
         dma((NY,)), dma((NY,)),
         dma((1, NX - 1)), dma((1, NX - 1)),
@@ -504,12 +530,9 @@
     def body(*refs):
         kernel(total_rows, *refs)
 
-    return pl.pallas_call(
+    margin, corrected = pl.pallas_call(
         body,
-        out_shape=(
-            jax.ShapeDtypeStruct((band, xrows), F32),
-            jax.ShapeDtypeStruct((rows, band), BF16),
-        ),
+        out_shape=(v((band, xrows), F32), v((rows, band), BF16)),
         in_specs=[pl.BlockSpec(memory_space=pl.ANY)],
         out_specs=(pl.BlockSpec(memory_space=pltpu.VMEM), pl.BlockSpec(memory_space=pltpu.VMEM)),
         scratch_shapes=scratch,
@@ -517,6 +540,28 @@
             collective_id=0, has_side_effects=True, vmem_limit_bytes=56 * 1024 * 1024
         ),
     )(orbitals)
+    return pl.pallas_call(
+        write_out,
+        out_shape=(
+            jax.ShapeDtypeStruct((band, xrows), F32),
+            jax.ShapeDtypeStruct((rows, band), BF16),
+        ),
+        in_specs=[pl.BlockSpec(memory_space=pltpu.VMEM)] * 2,
+        out_specs=(pl.BlockSpec(memory_space=pl.ANY),) * 2,
+        scratch_shapes=[dma((2,))],
+        compiler_params=pltpu.CompilerParams(vmem_limit_bytes=4 * 1024 * 1024),
+    )(margin, corrected)
+
+
+def write_out(m_ref, o_ref, m_out, o_out, sem):
+    copies = [
+        pltpu.make_async_copy(m_ref, m_out, sem.at[0]),
+        pltpu.make_async_copy(o_ref, o_out, sem.at[1]),
+    ]
+    for h in copies:
+        h.start()
+    for h in copies:
+        h.wait()
 
 
 def solution(mesh):

time: 130 us -> 122 us (0.938); the launches traced: 128 us -> 122 us
  local copies, waits for them, and re-layouts: 3.44 us -> 0 us
  Pallas kernels: 124 us -> 122 us
    unnamed x2 -> x0, local copies, waits for them, and re-layouts: 3.44 us -> none
    pallas_call x1 -> x2, Pallas kernels: 124 us -> 122 us  [the longest x1 121 us: shards(): pl.pallas_call(body, out_shape=(v((band, xrows), F32), v((rows, band), BF...]
where the time goes in v4:
time: 122 us
  Pallas kernels  122 us (100%)
    pallas_call x1, Pallas kernels, shards(): pl.pallas_call(body, out_shape=(v((band, xrows), F32), v((rows, band), BF...  121 us

profile of v4, /device:TPU:1, one launch (start us, length us, event | category | flops | bytes accessed | tf_op | source)
XLA Modules:
  0.0 122.1 jit_solution(16819143893421940399)
XLA Ops:
  0.6 120.7 %shard_map.30 = (f32[256,128]{1,0:T(8,128)S(1)}, bf16[1024,256]{1,0:T(8,128)(2,1)S(1)}) custom-call(bf16[1024,256]{1,0:T(8,128)(2,1)} %refs_0_.1), custom_call_target="tpu_custom_call" | custom-call | tf_op jit(solution)/shard_map/pallas_call | solution.py:533
  121.3 0.9 shard_map.31

commit v5 on v4

--- a/solution.py
+++ b/solution.py
@@ -10,7 +10,7 @@
 NY, NX, NZ = 8, 4, 8
 SLOT = (0, 1, 7, 2, 6, 4, 3, 5)
 POS = tuple(SLOT.index(k) for k in range(NY))
-GROUPS = ((0, 3), (3, 2), (6, 2), (5, 1))
+GROUPS = ((0, 1), (3, 2), (6, 2), (5, 1), (1, 2))
 FACTORS = ((0, 0), (1, 0), (7, 0), (2, 0), (6, 0), (2, 6), (3, 0), (5, 0))
 FAR = 5
 MESH_ID = pl.DeviceIdType.MESH
@@ -24,9 +24,9 @@
 
 def kernel(
     total_rows, x_hbm, m_out, o_out, xa, ph, xs, xr, zs, zr, db, d32, dq, dj, da, ca,
-    ms, mr, acc, osb, in_sem, sw_s, sw_r, ring_s, ring_r, sib_s, sib_r, x_s, x_r, z_s, z_r,
-    q_s, q_r, y_s, y_r, yf_s, yf_r, gx_s, gx_r, gz_s, gz_r, hz_s, hz_r, hx_s, hx_r,
-    ax_s, ax_r, az_s, az_r, bz_s, bz_r, bx_s, bx_r, m_s, m_r, out_s, out_r,
+    ms, mr, acc, osb, rb, land, in_sem, sw_s, sw_r, ring_s, ring_r, sib_s, sib_r, x_s, x_r, z_s, z_r,
+    q_s, q_r, y_s, y_r, yf_s, yf_r, gx_s, gx_r, gz_s, gz_r, hz_s, hz_r, hp_s, hp_r,
+    ax_s, ax_r, az_s, az_r, bz_s, bz_r, bx_s, bx_r, m_s, m_r, os_s, os_r, oz_s, oz_r,
 ):
     y = lax.axis_index("y")
     zl = lax.axis_index("zl")
@@ -38,7 +38,6 @@
     band = ph.shape[1]
     xrows = xs.shape[2]
     zrows = zs.shape[2]
-    sends = []
 
     def zdev(d):
         t = lax.rem(z + d + NZ, NZ)
@@ -58,9 +57,7 @@
         )
 
     def send(src, dst, ssem, rsem, dev):
-        h = copy(src, dst, ssem, rsem, dev)
-        h.start()
-        sends.append(h)
+        copy(src, dst, ssem, rsem, dev).start()
 
     def arrived(dst, ssem, rsem):
         copy(dst, dst, ssem, rsem, sibling).wait_recv()
@@ -71,7 +68,7 @@
     oth_in.start()
 
     barrier = pltpu.get_barrier_semaphore()
-    peers = [sibling, {"zl": 1 - zl, "c": 1 - c}]
+    peers = [sibling]
     peers += [ydev(d) for d in range(1, NY)]
     peers += [xdev(d) for d in range(1, NX)]
     peers += [zdev(d) for d in range(1, NZ)]
@@ -88,19 +85,19 @@
     def to_minus(k, j):
         t = xa.at[k, c, subs[j]]
         u = xa.at[k + 1, c, subs[j]]
-        send(t, u, ring_s.at[0, k, j], ring_r.at[0, k, j], ydev(-1))
+        send(t, u, ring_s, ring_r.at[0, k, j], ydev(-1))
 
     def to_plus(k, j):
         t = xa.at[(NY - k) % NY, c, subs[j]]
         u = xa.at[NY - k - 1, c, subs[j]]
-        send(t, u, ring_s.at[1, k, j], ring_r.at[1, k, j], ydev(1))
+        send(t, u, ring_s, ring_r.at[1, k, j], ydev(1))
 
     def to_sibling(k, j):
         t = xa.at[k, c, subs[j]]
-        send(t, t, sib_s.at[k, j], sib_r.at[k, j], sibling)
+        send(t, t, sib_s, sib_r.at[k, j], sibling)
 
     def from_sibling(k, j):
-        arrived(xa.at[k, 1 - c, subs[j]], sib_s.at[k, j], sib_r.at[k, j])
+        arrived(xa.at[k, 1 - c, subs[j]], sib_s, sib_r.at[k, j])
 
     def partial_margin(g, j):
         off, n = GROUPS[g]
@@ -116,22 +113,15 @@
             to = 2 * s + i
             d = lax.rem(to - x + NX, NX)
             at = jnp.maximum(d - 1, 0)
-            h = copy(xs.at[to, pl.ds(off, n)], xr.at[at, pl.ds(off, n)], x_s.at[g, at], x_r.at[g, at], {"x": to})
+            h = copy(xs.at[to, pl.ds(off, n)], xr.at[at, pl.ds(off, n)], x_s, x_r.at[g], {"x": to})
 
             @pl.when(d > 0)
             def _():
                 h.start()
 
-    def partial_sent(g):
-        off, n = GROUPS[g]
-        for d in range(1, NX):
-            t = xr.at[d - 1, pl.ds(off, n)]
-            copy(t, t, x_s.at[g, d - 1], x_r.at[g, d - 1], sibling).wait_send()
-
     def sum_over_x(g):
         off, n = GROUPS[g]
-        for d in range(1, NX):
-            arrived(xr.at[d - 1, pl.ds(off, n)], x_s.at[g, d - 1], x_r.at[g, d - 1])
+        arrived(xr.at[:, pl.ds(off, n)], x_s, x_r.at[g])
         for p in range(off, off + n):
             v = xs[x, p].astype(F32)
             for d in range(1, NX):
@@ -141,13 +131,12 @@
             t = lax.rem(z + d, NZ)
             send(
                 zs.at[t, pl.ds(off, n)], zr.at[d - 1, pl.ds(off, n)],
-                z_s.at[g, d - 1], z_r.at[g, d - 1], zdev(d),
+                z_s, z_r.at[g], zdev(d),
             )
 
     def sum_over_z(g):
         off, n = GROUPS[g]
-        for d in range(1, NZ):
-            arrived(zr.at[d - 1, pl.ds(off, n)], z_s.at[g, d - 1], z_r.at[g, d - 1])
+        arrived(zr.at[:, pl.ds(off, n)], z_s, z_r.at[g])
         for p in range(off, off + n):
             v = zs[z, p].astype(F32)
             for d in range(1, NZ):
@@ -181,12 +170,12 @@
         to_sibling(0, j)
     def ring_step(h, j):
         if h < 4 or j == 0:
-            arrived(xa.at[h, c, subs[j]], ring_s.at[0, h - 1, j], ring_r.at[0, h - 1, j])
+            arrived(xa.at[h, c, subs[j]], ring_s, ring_r.at[0, h - 1, j])
             if h < 3 or (h == 3 and j == 0):
                 to_minus(h, j)
             to_sibling(h, j)
         if h < 4 or j == 1:
-            arrived(xa.at[NY - h, c, subs[j]], ring_s.at[1, h - 1, j], ring_r.at[1, h - 1, j])
+            arrived(xa.at[NY - h, c, subs[j]], ring_s, ring_r.at[1, h - 1, j])
             if h < 3 or (h == 3 and j == 1):
                 to_plus(h, j)
             to_sibling(NY - h, j)
@@ -195,7 +184,7 @@
         off, n = GROUPS[g]
         v = da.at[pl.ds(off, n), z, x]
         for d in range(1, NX):
-            send(v, v, gx_s.at[g, d - 1], gx_r.at[g, d - 1], xdev(d))
+            send(v, v, gx_s, gx_r.at[g // 4], xdev(d))
 
     def slab(g, i, h):
         off, n = GROUPS[g]
@@ -205,13 +194,11 @@
     def hop_send(g, i, h):
         t, ps = slab(g, i, h - 1)
         v = da.at[ps, t] if h < 4 else da.at[ps, t, pl.ds(2 * i, 2)]
-        send(v, v, gz_s.at[g, i, h - 1], gz_r.at[g, i, h - 1], zdev(-1 if i == 0 else 1))
+        send(v, v, gz_s, gz_r.at[g // 4, i, h - 1], zdev(-1 if i == 0 else 1))
 
     def gather_z(g):
         off, n = GROUPS[g]
-        for d in range(1, NX):
-            t = lax.rem(x + NX - d, NX)
-            arrived(da.at[pl.ds(off, n), z, t], gx_s.at[g, d - 1], gx_r.at[g, d - 1])
+        arrived(da.at[pl.ds(off, n), z, pl.ds(0, NX - 1)], gx_s, gx_r.at[g // 4])
         for i in range(2):
             hop_send(g, i, 1)
 
@@ -219,7 +206,7 @@
         for i in range(2):
             t, ps = slab(g, i, h)
             v = da.at[ps, t] if h < 4 else da.at[ps, t, pl.ds(2 * i, 2)]
-            arrived(v, gz_s.at[g, i, h - 1], gz_r.at[g, i, h - 1])
+            arrived(v, gz_s, gz_r.at[g // 4, i, h - 1])
             if h < 4:
                 hop_send(g, i, h + 1)
 
@@ -227,22 +214,21 @@
         off, n = GROUPS[g]
         v = da.at[pl.ds(off, n), z, x]
         for d in range(1, NZ):
-            send(db.at[pl.ds(off, n)], v, hz_s.at[g - 1, d - 1], hz_r.at[g - 1, d - 1], zdev(d))
-
-    def near_x(g):
-        off, n = GROUPS[g]
-        for d in range(1, NZ):
-            t = lax.rem(z + NZ - d, NZ)
-            arrived(da.at[pl.ds(off, n), t, x], hz_s.at[g - 1, d - 1], hz_r.at[g - 1, d - 1])
-        v = da.at[pl.ds(off, n), :, x]
-        for d in range(1, NX):
-            send(v, v, hx_s.at[g - 1, d - 1], hx_r.at[g - 1, d - 1], xdev(d))
-
-    def near_done(g):
-        off, n = GROUPS[g]
-        for d in range(1, NX):
-            t = lax.rem(x + NX - d, NX)
-            arrived(da.at[pl.ds(off, n), :, t], hx_s.at[g - 1, d - 1], hx_r.at[g - 1, d - 1])
+            send(db.at[pl.ds(off, n)], v, hz_s, hz_r.at[g - 1, d - 1], zdev(d))
+
+    def pieces_x(g, rs):
+        off, n = GROUPS[g]
+        for r in rs:
+            t = lax.rem(z + r, NZ)
+            v = da.at[pl.ds(off, n), t, x]
+            if r:
+                arrived(v, hz_s, hz_r.at[g - 1, NZ - 1 - r])
+            for d in (1, 3, 2):
+                send(v if r else db.at[pl.ds(off, n)], v, hp_s, hp_r.at[g - 1], xdev(d))
+
+    def pieces_done(g):
+        off, n = GROUPS[g]
+        arrived(da.at[pl.ds(off, n), :, pl.ds(0, NX - 1)], hp_s, hp_r.at[g - 1])
 
     PARTS = ((0, 6), (6, 2))
 
@@ -253,18 +239,17 @@
     def left_send(i):
         ps = rows_part(i)
         for k in range(1, NY):
-            send(db.at[ps], dj.at[k, c, ps], y_s.at[i, k - 1], y_r.at[i, k - 1], ydev(-k))
+            send(db.at[ps], dj.at[k, c, ps], y_s, y_r, ydev(-k))
         off, n = PARTS[i]
         for p in range(off, off + n):
             dj[0, c, p] = db[p]
         if i == 1:
-            send(db, dj.at[0, c], yf_s.at[0], yf_r.at[0], sibling)
+            send(db, dj.at[0, c], yf_s, yf_r.at[0], sibling)
 
     def left_pass():
-        for k in range(1, NY):
-            for i in range(2):
-                arrived(dj.at[k, c, rows_part(i)], y_s.at[i, k - 1], y_r.at[i, k - 1])
-            send(dj.at[k, c], dj.at[k, c], yf_s.at[k], yf_r.at[k], sibling)
+        v = dj.at[pl.ds(1, NY - 1), c]
+        arrived(v, y_s, y_r)
+        send(v, v, yf_s, yf_r.at[1], sibling)
 
     def pair_in(h, j):
         from_sibling(h, j)
@@ -273,56 +258,72 @@
     ring_step(1, 0)
     from_sibling(0, 0)
     from_sibling(0, 1)
+    partial_margin(0, 0)
+    partial_margin(0, 1)
     pair_in(1, 0)
-    partial_margin(0, 0)
+    partial_margin(4, 0)
     ring_step(1, 1)
     pair_in(1, 1)
-    partial_margin(0, 1)
+    partial_margin(4, 1)
+    sum_over_x(0)
     ring_step(2, 0)
     pair_in(2, 0)
     partial_margin(1, 0)
-    sum_over_x(0)
+    sum_over_z(0)
+    gather_x(0)
     ring_step(2, 1)
+    sum_over_x(4)
     pair_in(2, 1)
     partial_margin(3, 0)
     partial_margin(3, 1)
     partial_margin(1, 1)
+    gather_z(0)
     ring_step(3, 0)
-    sum_over_z(0)
-    gather_x(0)
+    hop(0, 1)
+    sum_over_z(4)
+    gather_x(4)
     pair_in(3, 0)
     partial_margin(2, 0)
     sum_over_x(3)
     sum_over_x(1)
-    gather_z(0)
+    hop(0, 2)
     ring_step(3, 1)
+    gather_z(4)
     pair_in(3, 1)
     partial_margin(2, 1)
     sum_over_z(3)
     sum_over_z(1)
     near_z(1)
-    hop(0, 1)
+    pieces_x(1, (0,))
+    hop(0, 3)
+    hop(4, 1)
     sum_over_x(2)
     place_far()
     near_z(3)
+    pieces_x(3, (0,))
     left_send(0)
     ring_step(4, 0)
     ring_step(4, 1)
-    hop(0, 2)
-    near_x(1)
+    hop(0, 4)
+    pieces_x(1, (1, 7, 2, 6))
+    hop(4, 2)
+    pieces_x(1, (3, 5, 4))
+    pieces_x(3, (1, 7))
     sum_over_z(2)
     near_z(2)
+    pieces_x(2, (0,))
     left_send(1)
-    near_x(3)
-    hop(0, 3)
-    near_x(2)
-    hop(0, 4)
+    hop(4, 3)
+    pieces_x(3, (2, 6, 3, 5, 4))
+    pieces_x(2, (1, 7, 2, 6))
+    hop(4, 4)
+    pieces_x(2, (3, 5, 4))
     left_pass()
-    near_done(1)
-    near_done(3)
-    near_done(2)
-    for k in range(NY):
-        arrived(dj.at[k, 1 - c], yf_s.at[k], yf_r.at[k])
+    pieces_done(1)
+    pieces_done(3)
+    pieces_done(2)
+    arrived(dj.at[0, 1 - c], yf_s, yf_r.at[0])
+    arrived(dj.at[pl.ds(1, NY - 1), 1 - c], yf_s, yf_r.at[1])
 
     def piece(b, t, u):
         return ca.at[t, u, pl.ds(4 * b, 4)]
@@ -333,27 +334,27 @@
 
     def a_send(d, i, h):
         v = zpiece(0, lax.rem(x + NX - d, NX), i, h - 1, h == 4)
-        send(v, v, az_s.at[d, i, h - 1], az_r.at[d, i, h - 1], zdev(-1 if i == 0 else 1))
+        send(v, v, az_s, az_r.at[d, i, h - 1], zdev(-1 if i == 0 else 1))
 
     def a_hop(d, h):
         for i in range(2):
             v = zpiece(0, lax.rem(x + NX - d, NX), i, h, h == 4)
-            arrived(v, az_s.at[d, i, h - 1], az_r.at[d, i, h - 1])
+            arrived(v, az_s, az_r.at[d, i, h - 1])
             if h < 4:
                 a_send(d, i, h + 1)
 
     def b_send(i, h):
         v = zpiece(1, x, i, h - 1, h == 4)
-        send(v, v, bz_s.at[i, h - 1], bz_r.at[i, h - 1], zdev(-1 if i == 0 else 1))
+        send(v, v, bz_s, bz_r.at[i, h - 1], zdev(-1 if i == 0 else 1))
 
     def b_along_x(r):
         v = piece(1, lax.rem(z + r, NZ), x)
         for d in (1, 3, 2):
-            send(v, v, bx_s.at[r, d - 1], bx_r.at[r, d - 1], xdev(d))
+            send(v, v, bx_s, bx_r, xdev(d))
 
     def b_hop(h):
         for i in range(2):
-            arrived(zpiece(1, x, i, h, h == 4), bz_s.at[i, h - 1], bz_r.at[i, h - 1])
+            arrived(zpiece(1, x, i, h, h == 4), bz_s, bz_r.at[i, h - 1])
             if h < 4:
                 b_send(i, h + 1)
         if h < 4:
@@ -364,7 +365,7 @@
 
     def plane_gather(between, b_done):
         for d in (1, 3, 2):
-            send(piece(0, z, x), piece(0, z, x), ax_s.at[d - 1], ax_r.at[d - 1], xdev(d))
+            send(piece(0, z, x), piece(0, z, x), ax_s, ax_r.at[d - 1], xdev(d))
         for i in range(2):
             b_send(i, 1)
         for i in range(2):
@@ -373,7 +374,7 @@
         b_hop(1)
         for d in (1, 3, 2):
             u = lax.rem(x + NX - d, NX)
-            arrived(piece(0, z, u), ax_s.at[d - 1], ax_r.at[d - 1])
+            arrived(piece(0, z, u), ax_s, ax_r.at[d - 1])
             for i in range(2):
                 a_send(d, i, 1)
         a_hop(0, 1)
@@ -383,10 +384,7 @@
                 b_hop(h)
                 a_hop(0, h)
             else:
-                for r in (0, 1, 7, 2, 6, 3, 5, 4):
-                    for d in (1, 3, 2):
-                        v = piece(1, lax.rem(z + r, NZ), lax.rem(x + NX - d, NX))
-                        arrived(v, bx_s.at[r, d - 1], bx_r.at[r, d - 1])
+                arrived(ca.at[:, pl.ds(0, NX - 1), pl.ds(4, 4)], bx_s, bx_r)
                 b_done()
             for d in (1, 3, 2):
                 a_hop(d, h - 1)
@@ -425,30 +423,34 @@
         ms[...] = mirror(1 - c).astype(BF16)
         send(ms, mr, m_s, m_r, sibling)
 
+    home = zl == c
+    kept = pl.ds(pl.multiple_of(zl * half, half), half)
+    swapped = pl.ds(pl.multiple_of((1 - zl) * half, half), half)
+    to_pair = {"zl": 1 - zl}
+
     def product(part):
-        for cc in range(2):
+        for i, cc in enumerate((1 - c, c)):
             for p in range(4 * part, 4 * part + 4):
                 k = SLOT[p]
                 for s in range(2):
                     v = dot(xa[k, cc, s], rows_of(p, s))
                     if part == 1 and p == 4 and s == 0:
-                        acc[cc] = v
+                        acc[i] = v
                     else:
-                        acc[cc] += v
+                        acc[i] += v
             if part == 0:
-                osb[cc] = acc[cc].astype(BF16)
-                mine = (zl == c) & (c == cc)
-                to = copy(
-                    osb.at[cc], o_out.at[pl.ds(zl * half, half), :], out_s.at[cc], out_r.at[zl], {"zl": c, "c": cc}
-                )
-
-                @pl.when(jnp.logical_not(mine))
-                def _():
-                    to.start()
-
-                @pl.when(mine)
-                def _():
-                    o_out[pl.ds(pl.multiple_of(zl * half, half), half), :] = osb[cc]
+                osb[i] = acc[i].astype(BF16)
+                if i == 0:
+                    copy(osb.at[0], rb, os_s, os_r, sibling).start()
+                else:
+
+                    @pl.when(home)
+                    def _():
+                        o_out[kept, :] = osb[1]
+
+                    @pl.when(jnp.logical_not(home))
+                    def _():
+                        copy(osb.at[1], land, oz_s, oz_r, to_pair).start()
 
     def first_half():
         arrived(mr, m_s, m_r)
@@ -459,27 +461,47 @@
         product(1)
 
     plane_gather(margin_work, first_half)
+
+    @pl.when(home)
+    def _():
+        arrived(rb, os_s, os_r)
+        copy(rb, land, oz_s, oz_r, to_pair).start()
+
     product(0)
 
-    other = o_out.at[pl.ds((1 - zl) * half, half), :]
-    arrived(other, out_s.at[0], out_r.at[1 - zl])
-
-    @pl.when(zl != c)
+    low = pl.ds(0, NZ - 1)
+    three = pl.ds(0, NX - 1)
+    for v, sem in (
+        (ph, sw_s),
+        (xa.at[pl.ds(0, 7), :, 0], ring_s),
+        (xa.at[:, :, 0], sib_s),
+        (xr, x_s),
+        (zr, z_s),
+        (dq, q_s),
+        (dj.at[pl.ds(1, NY - 1), 0], y_s),
+        (dj.at[:, 0], yf_s),
+        (da.at[three, 0, three], gx_s),
+        (da.at[three, low], gz_s),
+        (da.at[pl.ds(0, 5), low, 0], hz_s),
+        (da.at[pl.ds(0, 5), :, three], hp_s),
+        (ca.at[0, three, pl.ds(0, 4)], ax_s),
+        (ca.at[low, :, pl.ds(0, 4)], az_s),
+        (ca.at[low, 0, pl.ds(0, 4)], bz_s),
+        (ca.at[:, three, pl.ds(0, 4)], bx_s),
+        (ms, m_s),
+    ):
+        copy(v, v, sem, m_r, sibling).wait_send()
+
+    @pl.when(jnp.logical_not(home))
     def _():
-        arrived(o_out.at[pl.ds(zl * half, half), :], out_s.at[0], out_r.at[zl])
-
-    for cc in range(2):
-
-        @pl.when(jnp.logical_not((zl == c) & (c == cc)))
-        def _():
-            copy(
-                osb.at[cc], o_out.at[pl.ds(zl * half, half), :], out_s.at[cc], out_r.at[zl], {"zl": c, "c": cc}
-            ).wait_send()
-
-    for g in range(len(GROUPS)):
-        partial_sent(g)
-    for h in sends:
-        h.wait_send()
+        arrived(rb, os_s, os_r)
+        o_out[kept, :] = rb[...]
+
+    arrived(land, oz_s, oz_r)
+    o_out[swapped, :] = land[...]
+
+    copy(rb, rb, os_s, os_r, sibling).wait_send()
+    copy(rb, rb, oz_s, oz_r, sibling).wait_send()
 
 
 def shards(total_rows, orbitals):
@@ -506,25 +528,28 @@
         v((xrows, band), BF16),
         v((2, half, band), F32),
         v((2, half, band), BF16),
+        v((half, band), BF16),
+        v((half, band), BF16),
         dma((2,)),
         dma, dma,
-        dma((2, 4, 2)), dma((2, 4, 2)),
-        dma((NY, 2)), dma((NY, 2)),
-        dma((4, NX - 1)), dma((4, NX - 1)),
-        dma((4, NZ - 1)), dma((4, NZ - 1)),
+        dma, dma((2, 4, 2)),
+        dma, dma((NY, 2)),
+        dma, dma((5,)),
+        dma, dma((5,)),
         dma, dma,
-        dma((2, NY - 1)), dma((2, NY - 1)),
-        dma((NY,)), dma((NY,)),
-        dma((1, NX - 1)), dma((1, NX - 1)),
-        dma((1, 2, 4)), dma((1, 2, 4)),
-        dma((3, NZ - 1)), dma((3, NZ - 1)),
-        dma((3, NX - 1)), dma((3, NX - 1)),
-        dma((NX - 1,)), dma((NX - 1,)),
-        dma((NX, 2, 4)), dma((NX, 2, 4)),
-        dma((2, 4)), dma((2, 4)),
-        dma((NZ, NX - 1)), dma((NZ, NX - 1)),
         dma, dma,
-        dma((2,)), dma((2,)),
+        dma, dma((2,)),
+        dma, dma((2,)),
+        dma, dma((2, 2, 4)),
+        dma, dma((3, NZ - 1)),
+        dma, dma((3,)),
+        dma, dma((NX - 1,)),
+        dma, dma((NX, 2, 4)),
+        dma, dma((2, 4)),
+        dma, dma,
+        dma, dma,
+        dma, dma,
+        dma, dma,
     ]
 
     def body(*refs):

time: 122 us -> 117 us (0.959)
  Pallas kernels: 122 us -> 116 us
    pallas_call x1, Pallas kernels: 121 us -> 115 us  [shards(): pl.pallas_call(body, out_shape=(v((band, xrows), F32), v((rows, band), BF...]
where the time goes in v5:
time: 117 us
  Pallas kernels  116 us (99%)
    pallas_call x1, Pallas kernels, shards(): pl.pallas_call(body, out_shape=(v((band, xrows), F32), v((rows, band), BF...  115 us

profile of v5, /device:TPU:1, one launch (start us, length us, event | category | flops | bytes accessed | tf_op | source)
XLA Modules:
  0.0 116.7 jit_solution(378909743167227401)
XLA Ops:
  0.6 115.2 %shard_map.30 = (f32[256,128]{1,0:T(8,128)S(1)}, bf16[1024,256]{1,0:T(8,128)(2,1)S(1)}) custom-call(bf16[1024,256]{1,0:T(8,128)(2,1)} %refs_0_.1), custom_call_target="tpu_custom_call" | custom-call | tf_op jit(solution)/shard_map/pallas_call | solution.py:558
  115.8 0.9 shard_map.31

commit v6 on v5

--- a/solution.py
+++ b/solution.py
@@ -13,6 +13,7 @@
 GROUPS = ((0, 1), (3, 2), (6, 2), (5, 1), (1, 2))
 FACTORS = ((0, 0), (1, 0), (7, 0), (2, 0), (6, 0), (2, 6), (3, 0), (5, 0))
 FAR = 5
+HALVES = ((0, 3), (3, 5))
 MESH_ID = pl.DeviceIdType.MESH
 F32 = jnp.float32
 BF16 = jnp.bfloat16
@@ -326,11 +327,16 @@
     arrived(dj.at[pl.ds(1, NY - 1), 1 - c], yf_s, yf_r.at[1])
 
     def piece(b, t, u):
-        return ca.at[t, u, pl.ds(4 * b, 4)]
+        off, n = HALVES[b]
+        return ca.at[t, u, pl.ds(off, n)]
 
     def zpiece(b, u, i, h, far):
+        off, n = HALVES[b]
+        first = (n + 1) // 2
         t = lax.rem(z + (h if i == 0 else NZ - h), NZ)
-        return ca.at[t, u, pl.ds(4 * b + 2 * i, 2)] if far else piece(b, t, u)
+        if not far:
+            return piece(b, t, u)
+        return ca.at[t, u, pl.ds(off, first) if i == 0 else pl.ds(off + first, n - first)]
 
     def a_send(d, i, h):
         v = zpiece(0, lax.rem(x + NX - d, NX), i, h - 1, h == 4)
@@ -382,12 +388,13 @@
         for h in range(2, 6):
             if h < 5:
                 b_hop(h)
-                a_hop(0, h)
             else:
-                arrived(ca.at[:, pl.ds(0, NX - 1), pl.ds(4, 4)], bx_s, bx_r)
+                arrived(ca.at[:, pl.ds(0, NX - 1), pl.ds(*HALVES[1])], bx_s, bx_r)
                 b_done()
             for d in (1, 3, 2):
                 a_hop(d, h - 1)
+            if h < 5:
+                a_hop(0, h)
 
     def rows_of(p, s):
         return jnp.concatenate([ca[:, 2 * s + i, p].reshape(xrows, band) for i in range(2)], axis=0)
@@ -430,14 +437,15 @@
 
     def product(part):
         for i, cc in enumerate((1 - c, c)):
-            for p in range(4 * part, 4 * part + 4):
-                k = SLOT[p]
-                for s in range(2):
-                    v = dot(xa[k, cc, s], rows_of(p, s))
-                    if part == 1 and p == 4 and s == 0:
-                        acc[i] = v
-                    else:
-                        acc[i] += v
+            tile = half // 2
+            for m in range(2):
+                rows = pl.ds(m * tile, tile)
+                v = None
+                for p in range(HALVES[part][0], sum(HALVES[part])):
+                    for s in range(2):
+                        w = dot(xa[SLOT[p], cc, s, rows], rows_of(p, s))
+                        v = w if v is None else v + w
+                acc[i, rows] = v if part == 1 else acc[i, rows] + v
             if part == 0:
                 osb[i] = acc[i].astype(BF16)
                 if i == 0:
@@ -484,10 +492,10 @@
         (da.at[three, low], gz_s),
         (da.at[pl.ds(0, 5), low, 0], hz_s),
         (da.at[pl.ds(0, 5), :, three], hp_s),
-        (ca.at[0, three, pl.ds(0, 4)], ax_s),
-        (ca.at[low, :, pl.ds(0, 4)], az_s),
-        (ca.at[low, 0, pl.ds(0, 4)], bz_s),
-        (ca.at[:, three, pl.ds(0, 4)], bx_s),
+        (ca.at[0, three, pl.ds(*HALVES[0])], ax_s),
+        (ca.at[low, :, pl.ds(*HALVES[0])], az_s),
+        (ca.at[low, 0, pl.ds(*HALVES[1])], bz_s),
+        (ca.at[:, three, pl.ds(*HALVES[1])], bx_s),
         (ms, m_s),
     ):
         copy(v, v, sem, m_r, sibling).wait_send()

time: 117 us -> 114 us (0.974)
  Pallas kernels: 116 us -> 113 us
    pallas_call x1, Pallas kernels: 115 us -> 113 us  [shards(): pl.pallas_call(body, out_shape=(v((band, xrows), F32), v((rows, band), BF...]
where the time goes in v6:
time: 114 us
  Pallas kernels  113 us (99%)
    pallas_call x1, Pallas kernels, shards(): pl.pallas_call(body, out_shape=(v((band, xrows), F32), v((rows, band), BF...  113 us

profile of v6, /device:TPU:1, one launch (start us, length us, event | category | flops | bytes accessed | tf_op | source)
XLA Modules:
  0.0 114.1 jit_solution(6396922426926280156)
XLA Ops:
  0.6 112.6 %shard_map.30 = (f32[256,128]{1,0:T(8,128)S(1)}, bf16[1024,256]{1,0:T(8,128)(2,1)S(1)}) custom-call(bf16[1024,256]{1,0:T(8,128)(2,1)} %refs_0_.1), custom_call_target="tpu_custom_call" | custom-call | tf_op jit(solution)/shard_map/pallas_call | solution.py:566
  113.2 0.9 shard_map.31

commit v7 on v6

--- a/solution.py
+++ b/solution.py
@@ -305,24 +305,22 @@
     left_send(0)
     ring_step(4, 0)
     ring_step(4, 1)
-    hop(0, 4)
     pieces_x(1, (1, 7, 2, 6))
     hop(4, 2)
     pieces_x(1, (3, 5, 4))
-    pieces_x(3, (1, 7))
     sum_over_z(2)
     near_z(2)
     pieces_x(2, (0,))
     left_send(1)
+    pieces_x(3, (1, 7, 2, 6))
     hop(4, 3)
-    pieces_x(3, (2, 6, 3, 5, 4))
-    pieces_x(2, (1, 7, 2, 6))
+    pieces_x(3, (3, 5, 4))
+    pieces_x(2, (1, 7, 2, 6, 3, 5, 4))
+    hop(0, 4)
     hop(4, 4)
-    pieces_x(2, (3, 5, 4))
     left_pass()
     pieces_done(1)
     pieces_done(3)
-    pieces_done(2)
     arrived(dj.at[0, 1 - c], yf_s, yf_r.at[0])
     arrived(dj.at[pl.ds(1, NY - 1), 1 - c], yf_s, yf_r.at[1])
 
@@ -403,7 +401,9 @@
         return jnp.concatenate([da[p, :, 2 * s + i].reshape(xrows, band) for i in range(2)], axis=0)
 
     acc_sq = [None] * NY
-    for k in range(NY):
+    for k in SLOT:
+        if POS[k] == GROUPS[2][0]:
+            pieces_done(2)
         left = [dj[k, s].reshape(NY * zrows, band) for s in range(2)]
         part = dot(left[0], dev_rows(POS[k], 0)) + dot(left[1], dev_rows(POS[k], 1))
         for p in range(NY):

time: 114 us -> 113 us (level)
  no operation moved by 1% of the time
where the time goes in v7:
time: 113 us
  Pallas kernels  112 us (99%)
    pallas_call x1, Pallas kernels, shards(): pl.pallas_call(body, out_shape=(v((band, xrows), F32), v((rows, band), BF...  111 us

profile of v7, /device:TPU:1, one launch (start us, length us, event | category | flops | bytes accessed | tf_op | source)
XLA Modules:
  0.0 113.0 jit_solution(7837016702218388325)
XLA Ops:
  0.6 111.5 %shard_map.30 = (f32[256,128]{1,0:T(8,128)S(1)}, bf16[1024,256]{1,0:T(8,128)(2,1)S(1)}) custom-call(bf16[1024,256]{1,0:T(8,128)(2,1)} %refs_0_.1), custom_call_target="tpu_custom_call" | custom-call | tf_op jit(solution)/shard_map/pallas_call | solution.py:566
  112.1 0.9 shard_map.31

commit v8 on v7

--- a/solution.py
+++ b/solution.py
@@ -445,20 +445,23 @@
                     for s in range(2):
                         w = dot(xa[SLOT[p], cc, s, rows], rows_of(p, s))
                         v = w if v is None else v + w
-                acc[i, rows] = v if part == 1 else acc[i, rows] + v
-            if part == 0:
-                osb[i] = acc[i].astype(BF16)
+                if part == 1:
+                    acc[i, rows] = v
+                    continue
+                osb[i, rows] = (acc[i, rows] + v).astype(BF16)
                 if i == 0:
-                    copy(osb.at[0], rb, os_s, os_r, sibling).start()
+                    copy(osb.at[0, rows], rb.at[rows], os_s, os_r, sibling).start()
                 else:
-
-                    @pl.when(home)
-                    def _():
-                        o_out[kept, :] = osb[1]
 
                     @pl.when(jnp.logical_not(home))
                     def _():
-                        copy(osb.at[1], land, oz_s, oz_r, to_pair).start()
+                        copy(osb.at[1, rows], land.at[rows], oz_s, oz_r, to_pair).start()
+
+        if part == 0:
+
+            @pl.when(home)
+            def _():
+                o_out[kept, :] = osb[1]
 
     def first_half():
         arrived(mr, m_s, m_r)

time: 113 us -> 114 us (level)
  no operation moved by 1% of the time
where the time goes in v8:
time: 114 us
  Pallas kernels  113 us (99%)
    pallas_call x1, Pallas kernels, shards(): pl.pallas_call(body, out_shape=(v((band, xrows), F32), v((rows, band), BF...  112 us

profile of v8, /device:TPU:1, one launch (start us, length us, event | category | flops | bytes accessed | tf_op | source)
XLA Modules:
  0.0 113.7 jit_solution(1925814437419733133)
XLA Ops:
  0.6 112.2 %shard_map.30 = (f32[256,128]{1,0:T(8,128)S(1)}, bf16[1024,256]{1,0:T(8,128)(2,1)S(1)}) custom-call(bf16[1024,256]{1,0:T(8,128)(2,1)} %refs_0_.1), custom_call_target="tpu_custom_call" | custom-call | tf_op jit(solution)/shard_map/pallas_call | solution.py:569
  112.8 0.9 shard_map.31
